TPU v7x, 8 devices: a whole 2x2x1 slice. The times are simulated.
8 devices in a mesh: dp: 2 (over z, y), tp: 4 (over x, core).
Axes of the slice: x: 2, y: 2, z: 1, core: 2. Of those that a mesh axis runs over, the one named last changes fastest.
Arguments:
- tokens: int32 [64], P('dp'), parts along dimension 0
- positions: int32 [64], P('dp'), parts along dimension 0
- self_keys: bfloat16 [2, 64, 448, 12, 64], P(None, 'dp', None, 'tp'), parts along dimension 1
- self_vals: bfloat16 [2, 64, 448, 12, 64], P(None, 'dp', None, 'tp'), parts along dimension 1
- cross_keys: bfloat16 [2, 64, 1500, 12, 64], P(None, 'dp', None, 'tp'), parts along dimension 1
- cross_vals: bfloat16 [2, 64, 1500, 12, 64], P(None, 'dp', None, 'tp'), parts along dimension 1
- embed_table: bfloat16 [52224, 768], P('tp')
- pos_table: bfloat16 [448, 768], replicated
- w_qkv: bfloat16 [2, 768, 3, 12, 64], P(None, None, None, 'tp')
- w_cq: bfloat16 [2, 768, 12, 64], P(None, None, 'tp')
- in_bias: float32 [2, 3, 12, 64], P(None, None, 'tp')
- w_out: bfloat16 [2, 2, 12, 64, 768], P(None, None, 'tp')
- out_bias: float32 [2, 3, 768], replicated
- w_fc1: bfloat16 [2, 768, 3072], P(None, None, 'tp')
- b_fc1: float32 [2, 3072], P(None, 'tp')
- w_fc2: bfloat16 [2, 3072, 768], P(None, 'tp')
- ln_layers: float32 [2, 3, 2, 768], replicated
- ln_final: float32 [2, 768], replicated
Outputs:
- output 1: float32 [64, 52224], P('dp', 'tp'), parts along dimension 0
- output 2: bfloat16 [2, 64, 448, 12, 64], P(None, 'dp', None, 'tp'), parts along dimension 1
- output 3: bfloat16 [2, 64, 448, 12, 64], P(None, 'dp', None, 'tp'), parts along dimension 1
There are 2 independent parts. A program takes and returns all parts, laid end to end along the dimension named above; an argument that names none is the same for every part.
All inputs are finite; a program needn't handle non-finite values.
Results may differ from a plain program's by a relative error of at most 0.0121347.
Values are sent between devices in bfloat16 or wider.
A program may use at most 1 GiB of HBM per device.

v0:
```python
import jax
import jax.numpy as jnp
from jax import lax
from jax.sharding import PartitionSpec as P


def layer_norm(residual, ln_gain, ln_shift):
    row_mean = jnp.mean(residual, axis=-1, keepdims=True)
    centred = residual - row_mean
    variance = jnp.mean(centred * centred, axis=-1, keepdims=True)
    return (centred * lax.rsqrt(variance + 1e-5) * ln_gain + ln_shift).astype(jnp.bfloat16)


def cross_attend(queries, key_rows, val_rows):
    scores = jnp.einsum('bhe,bthe->bht', queries, key_rows, preferred_element_type=jnp.float32) * (queries.shape[-1] ** -0.5)
    weights = jax.nn.softmax(scores, axis=-1).astype(jnp.bfloat16)
    return jnp.einsum('bht,bthe->bhe', weights, val_rows, preferred_element_type=jnp.float32).astype(jnp.bfloat16)


def self_attend(queries, key_new, val_new, cache_keys, cache_vals, mask_add):
    qk_scale = queries.shape[-1] ** -0.5
    past_scores = jnp.einsum('bhe,bthe->bht', queries, cache_keys, preferred_element_type=jnp.float32) * qk_scale + mask_add
    new_score = jnp.einsum('bhe,bhe->bh', queries, key_new, preferred_element_type=jnp.float32)[:, :, None] * qk_scale
    score_peak = jnp.maximum(jnp.max(past_scores, axis=-1, keepdims=True), new_score)
    past_exp = jnp.exp(past_scores - score_peak)
    new_exp = jnp.exp(new_score - score_peak)
    denominator = jnp.sum(past_exp, axis=-1, keepdims=True) + new_exp
    past_weight = (past_exp / denominator).astype(jnp.bfloat16)
    new_weight = (new_exp / denominator).astype(jnp.bfloat16)
    mixed_vals = jnp.einsum('bht,bthe->bhe', past_weight, cache_vals, preferred_element_type=jnp.float32)
    mixed_vals = mixed_vals + new_weight.astype(jnp.float32) * val_new.astype(jnp.float32)
    return mixed_vals.astype(jnp.bfloat16)


def group_sum(part_sum):
    return lax.psum(part_sum, 'tp').astype(jnp.bfloat16).astype(jnp.float32)


def solution(mesh):
    def local_step(tokens, positions, self_keys, self_vals, cross_keys, cross_vals, embed_table, pos_table, w_qkv, w_cq, in_bias, w_out, out_bias, w_fc1, b_fc1, w_fc2, ln_layers, ln_final):
        shard_rows = embed_table.shape[0]
        local_ids = tokens - lax.axis_index('tp') * shard_rows
        owned_mask = (local_ids >= 0) & (local_ids < shard_rows)
        picked = jnp.take(embed_table, jnp.clip(local_ids, 0, shard_rows - 1), axis=0)
        picked = jnp.where(owned_mask[:, None], picked, jnp.zeros_like(picked))
        residual = lax.psum(picked, 'tp').astype(jnp.float32) + jnp.take(pos_table, positions, axis=0).astype(jnp.float32)
        cache_pos = jnp.arange(self_keys.shape[2])[None, :]
        mask_add = jnp.where(cache_pos < positions[:, None], 0.0, -1e30)[:, None, :]
        new_key_rows = []
        new_val_rows = []
        for layer_idx in range(self_keys.shape[0]):
            ln_params = ln_layers[layer_idx]
            bias_in = in_bias[layer_idx]
            hidden = layer_norm(residual, ln_params[0, 0], ln_params[0, 1])
            projected = jnp.einsum('bd,dthe->bthe', hidden, w_qkv[layer_idx], preferred_element_type=jnp.float32)
            queries = (projected[:, 0] + bias_in[0]).astype(jnp.bfloat16)
            key_new = projected[:, 1].astype(jnp.bfloat16)
            val_new = (projected[:, 2] + bias_in[1]).astype(jnp.bfloat16)
            attended = self_attend(queries, key_new, val_new, self_keys[layer_idx], self_vals[layer_idx], mask_add)
            head_sum = jnp.einsum('bhe,hed->bd', attended, w_out[layer_idx, 0], preferred_element_type=jnp.float32)
            residual = residual + group_sum(head_sum) + out_bias[layer_idx, 0]
            hidden = layer_norm(residual, ln_params[1, 0], ln_params[1, 1])
            cross_q = (jnp.einsum('bd,dhe->bhe', hidden, w_cq[layer_idx], preferred_element_type=jnp.float32) + bias_in[2]).astype(jnp.bfloat16)
            attended = cross_attend(cross_q, cross_keys[layer_idx], cross_vals[layer_idx])
            head_sum = jnp.einsum('bhe,hed->bd', attended, w_out[layer_idx, 1], preferred_element_type=jnp.float32)
            residual = residual + group_sum(head_sum) + out_bias[layer_idx, 1]
            hidden = layer_norm(residual, ln_params[2, 0], ln_params[2, 1])
            fc1_out = jnp.dot(hidden, w_fc1[layer_idx], preferred_element_type=jnp.float32) + b_fc1[layer_idx]
            active = jax.nn.gelu(fc1_out, approximate=False).astype(jnp.bfloat16)
            fc2_out = jnp.dot(active, w_fc2[layer_idx], preferred_element_type=jnp.float32)
            residual = residual + group_sum(fc2_out) + out_bias[layer_idx, 2]
            new_key_rows.append(key_new)
            new_val_rows.append(val_new)
        final_hidden = layer_norm(residual, ln_final[0], ln_final[1])
        logits = jnp.einsum('bd,vd->bv', final_hidden, embed_table, preferred_element_type=jnp.float32)
        write_mask = (cache_pos == positions[:, None])[None, :, :, None, None]
        new_keys = jnp.where(write_mask, jnp.stack(new_key_rows)[:, :, None], self_keys)
        new_vals = jnp.where(write_mask, jnp.stack(new_val_rows)[:, :, None], self_vals)
        return logits, new_keys, new_vals

    batch_spec = P('dp')
    cache_spec = P(None, 'dp', None, 'tp', None)
    in_specs = (batch_spec, batch_spec, cache_spec, cache_spec, cache_spec, cache_spec, P('tp', None), P(None, None), P(None, None, None, 'tp', None), P(None, None, 'tp', None), P(None, None, 'tp', None), P(None, None, 'tp', None, None), P(None, None, None), P(None, None, 'tp'), P(None, 'tp'), P(None, 'tp', None), P(None, None, None, None), P(None, None))
    out_specs = (P('dp', 'tp'), cache_spec, cache_spec)
    return jax.shard_map(local_step, mesh=mesh, in_specs=in_specs, out_specs=out_specs, check_vma=False)
```

profile of v0, /device:TPU:0, one launch (start us, length us, event | category | flops | bytes accessed | tf_op | source)
XLA Modules:
  0.0 190.5 jit_solution(13594586329407637223)
XLA Ops:
  0.7 0.7 compare_and_fusion.1
  1.4 9.9 %gather_fusion = bf16[32,768]{1,0:T(8,128)(2,1)S(1)} fusion(bf16[13056,768]{1,0:T(8,128)(2,1)} %param.24, s32[1024]{0:T(1024)S(1)} %pad_clamp_fusion.1), kind=kCustom, calls=%fused_computation | custom fusion | bytes 98432 | tf_op jit(solution)/shard_map/jit(_take)/gather | solution.py:44
  11.4 13.6 %psum.49 = bf16[32,768]{1,0:T(8,128)(2,1)S(1)} all-reduce(bf16[32,768]{1,0:T(8,128)(2,1)S(1)} %select_select_fusion), channel_id=1, replica_groups=mesh['dp'=2,'tp'=4] {'tp'}, use_global_device_ids=true, to_apply=%region_0.1 | all-reduce | flops 24576 | bytes 98304 | tf_op jit(solution)/shard_map/psum | solution.py:46
  25.1 0.7 compare_select_fusion
  25.7 0.6 gather_fusion.1
  26.4 0.7 compare_and_fusion
  27.0 0.2 fusion.122
  27.2 0.2 multiply_reduce_fusion.6
  27.4 0.8 slice_bitcast_fusion.2
  28.2 1.7 fusion.62
  29.9 0.8 fusion.331
  30.9 3.8 %fusion.22 = f32[32,3,1,448]{3,2,1,0:T(1,128)S(1)} fusion(bf16[2,32,448,3,64]{2,4,3,1,0:T(8,128)(2,1)} %param.20, bf16[32,3,64,1]{2,0,1,3:T(8,128)(2,1)S(1)} %get-tuple-element.42), kind=kOutput, calls=%fused_computation.26 | convolution fusion | flops 5505024 | bytes 6475776 | tf_op jit(solution)/shard_map/bhe,bthe->bht/dot_general | solution.py:22
  34.9 0.2 fusion.88
  35.2 4.5 %fusion.20 = f32[32,3,1,64]{3,2,1,0:T(1,128)S(1)} fusion(bf16[2,32,448,3,64]{2,4,3,1,0:T(8,128)(2,1)} %param.21, bf16[32,3,448,1]{2,0,1,3:T(8,128)(2,1)S(1)} %fusion.120), kind=kOutput, calls=%fused_computation.24 | convolution fusion | flops 5505024 | bytes 6402048 | tf_op jit(solution)/shard_map/bht,bthe->bhe/dot_general | solution.py:30
  39.7 0.3 convolution_bitcast_fusion.3
  40.0 11.1 %psum.50 = bf16[32,768]{1,0:T(8,128)(2,1)S(1)} all-reduce(f32[32,768]{1,0:T(8,128)S(1)} %convolution_bitcast_fusion.3), channel_id=1, replica_groups=mesh['dp'=2,'tp'=4] {'tp'}, use_global_device_ids=true, to_apply=%region_5.6 | all-reduce | flops 24576 | bytes 147456 | tf_op jit(solution)/shard_map/psum | solution.py:36
  51.2 0.2 fusion.330
  51.4 0.2 multiply_reduce_fusion.5
  51.6 0.3 fusion.59
  51.9 7.7 %fusion.10 = f32[32,3,1,1500]{3,2,1,0:T(1,128)S(1)} fusion(bf16[2,32,1500,3,64]{2,4,3,1,0:T(8,128)(2,1)} %param.22, bf16[32,3,64,1]{2,0,1,3:T(8,128)(2,1)S(1)} %fusion.59), kind=kOutput, calls=%fused_computation.12 | convolution fusion | flops 18432000 | bytes 19462656 | tf_op jit(solution)/shard_map/bhe,bthe->bht/dot_general | solution.py:15
  59.6 0.3 fusion.36
  59.9 8.9 %fusion.8 = bf16[32,3,1,64]{3,2,1,0:T(2,128)(2,1)S(1)} fusion(bf16[2,32,1500,3,64]{2,4,3,1,0:T(8,128)(2,1)} %param.23, bf16[32,3,1500,1]{2,0,1,3:T(8,128)(2,1)S(1)} %fusion.36), kind=kOutput, calls=%fused_computation.10 | convolution fusion | flops 18432000 | bytes 19174656 | tf_op jit(solution)/shard_map/bht,bthe->bhe/dot_general | solution.py:17
  68.8 0.2 convolution_bitcast_fusion.2
  69.0 11.2 %psum.51 = bf16[32,768]{1,0:T(8,128)(2,1)S(1)} all-reduce(f32[32,768]{1,0:T(8,128)S(1)} %convolution_bitcast_fusion.2), channel_id=1, replica_groups=mesh['dp'=2,'tp'=4] {'tp'}, use_global_device_ids=true, to_apply=%region_10.11 | all-reduce | flops 24576 | bytes 147456 | tf_op jit(solution)/shard_map/psum | solution.py:36
  80.4 0.2 multiply_reduce_fusion.4
  80.6 2.3 %fusion.42 = f32[32,768]{1,0:T(8,128)S(1)} fusion(bf16[2,768,768]{2,1,0:T(8,128)(2,1)} %param.33, bf16[2,768,768]{2,1,0:T(8,128)(2,1)} %param.31, f32[32,768]{1,0:T(8,128)S(1)} %get-tuple-element.34, f32[768]{0:T(1024)S(1)} %get-tuple-element.24, f32[768]{0:T(1024)S(1)} %get-tuple-element.16, f32[768]{0:T(1024)S(1)} %get-tuple-element.15, ...), kind=kOutput, calls=%fused_computation.46 | convolution fusion | flops 77242368 | bytes 2565376 | tf_op jit(solution)/shard_map/dot_general | solution.py:70
  82.9 11.2 %psum.52 = bf16[32,768]{1,0:T(8,128)(2,1)S(1)} all-reduce(f32[32,768]{1,0:T(8,128)S(1)} %fusion.42), channel_id=1, replica_groups=mesh['dp'=2,'tp'=4] {'tp'}, use_global_device_ids=true, to_apply=%region_13.14 | all-reduce | flops 24576 | bytes 147456 | tf_op jit(solution)/shard_map/psum | solution.py:36
  94.3 0.2 multiply_reduce_fusion.3
  94.6 1.8 fusion.60
  96.8 20.6 %broadcast_select_fusion = (bf16[2,32,448,3,64]{2,4,3,1,0:T(8,128)(2,1)}, bf16[2,32,448,3,64]{2,4,3,1,0:T(8,128)(2,1)}) fusion(bf16[2,32,448,3,64]{2,4,3,1,0:T(8,128)(2,1)} %param.21, pred[32,448]{1,0:T(8,128)(4,1)S(1)} %iota_compare_fusion, bf16[2,32,3,64]{3,2,1,0:T(4,128)(2,1)S(1)} %copy.34, bf16[2,32,448,3,64]{2,4,3,1,0:T(8,128)(2,1)} %param.20, ...), kind=kLoop, calls=%fused_computation.18 | loop fusion | flops 11010048 | bytes 44103680 | tf_op jit(solution)/shard_map/jit(_where)/select_n | solution.py:78
  117.5 0.9 fusion.18
  118.5 0.2 fusion.89
  118.9 0.9 slice-done.5
  119.8 1.7 fusion.16
  121.5 0.3 convolution_bitcast_fusion.1
  121.8 11.4 %psum.53 = bf16[32,768]{1,0:T(8,128)(2,1)S(1)} all-reduce(f32[32,768]{1,0:T(8,128)S(1)} %convolution_bitcast_fusion.1), channel_id=1, replica_groups=mesh['dp'=2,'tp'=4] {'tp'}, use_global_device_ids=true, to_apply=%region_18.19 | all-reduce | flops 24576 | bytes 147456 | tf_op jit(solution)/shard_map/psum | solution.py:36
  133.3 0.2 multiply_reduce_fusion.2
  133.5 0.3 fusion.58
  133.8 7.7 %fusion.6 = f32[32,3,1,1500]{3,2,1,0:T(1,128)S(1)} fusion(bf16[2,32,1500,3,64]{2,4,3,1,0:T(8,128)(2,1)} %param.22, bf16[32,3,64,1]{2,0,1,3:T(8,128)(2,1)S(1)} %fusion.58), kind=kOutput, calls=%fused_computation.8 | convolution fusion | flops 18432000 | bytes 19462656 | tf_op jit(solution)/shard_map/bhe,bthe->bht/dot_general | solution.py:15
  141.5 0.3 fusion.37
  141.8 8.9 %fusion.4 = bf16[32,3,1,64]{3,2,1,0:T(2,128)(2,1)S(1)} fusion(bf16[2,32,1500,3,64]{2,4,3,1,0:T(8,128)(2,1)} %param.23, bf16[32,3,1500,1]{2,0,1,3:T(8,128)(2,1)S(1)} %fusion.37), kind=kOutput, calls=%fused_computation.6 | convolution fusion | flops 18432000 | bytes 19174656 | tf_op jit(solution)/shard_map/bht,bthe->bhe/dot_general | solution.py:17
  150.7 0.2 convolution_bitcast_fusion
  150.9 11.4 %psum.54 = bf16[32,768]{1,0:T(8,128)(2,1)S(1)} all-reduce(f32[32,768]{1,0:T(8,128)S(1)} %convolution_bitcast_fusion), channel_id=1, replica_groups=mesh['dp'=2,'tp'=4] {'tp'}, use_global_device_ids=true, to_apply=%region_23.24 | all-reduce | flops 24576 | bytes 147456 | tf_op jit(solution)/shard_map/psum | solution.py:36
  162.5 0.2 multiply_reduce_fusion.1
  162.7 2.4 %fusion.38 = f32[32,768]{1,0:T(8,128)S(1)} fusion(bf16[2,768,768]{2,1,0:T(8,128)(2,1)} %param.33, bf16[2,768,768]{2,1,0:T(8,128)(2,1)} %param.31, f32[32,768]{1,0:T(8,128)S(1)} %get-tuple-element.28, f32[768]{0:T(1024)S(1)} %get-tuple-element.23, f32[768]{0:T(1024)S(1)} %get-tuple-element.4, f32[768]{0:T(1024)S(1)} %get-tuple-element.3, ...), kind=kOutput, calls=%fused_computation.42 | convolution fusion | flops 77242368 | bytes 2565376 | tf_op jit(solution)/shard_map/dot_general | solution.py:70
  165.1 11.1 %psum.55 = bf16[32,768]{1,0:T(8,128)(2,1)S(1)} all-reduce(f32[32,768]{1,0:T(8,128)S(1)} %fusion.38), channel_id=1, replica_groups=mesh['dp'=2,'tp'=4] {'tp'}, use_global_device_ids=true, to_apply=%region_26.27 | all-reduce | flops 24576 | bytes 147456 | tf_op jit(solution)/shard_map/psum | solution.py:36
  176.3 0.2 multiply_reduce_fusion
  176.6 13.9 %fusion.132 = f32[32,13056]{1,0:T(8,128)} fusion(bf16[13056,768]{1,0:T(8,128)(2,1)} %param.24, f32[32,768]{1,0:T(8,128)S(1)} %get-tuple-element.26, f32[768]{0:T(1024)S(1)} %get-tuple-element.22, f32[768]{0:T(1024)S(1)} %get-tuple-element.21, f32[32]{0:T(128)S(1)} %add_rsqrt_fusion, f32[32]{0:T(128)S(1)} %broadcast_multiply_fusion), kind=kOutput, calls=%fused_computation.175 | convolution fusion | flops 641851392 | bytes 21829888 | tf_op jit(solution)/shard_map/bd,vd->bv/dot_general | solution.py:75
  (80 shorter events, 2.1 us)
Async XLA Ops:
  0.6 25.1 %copy-start = (bf16[448,768]{1,0:T(8,128)(2,1)S(1)}, bf16[448,768]{1,0:T(8,128)(2,1)}, u32[]{:S(2)}) copy-start(bf16[448,768]{1,0:T(8,128)(2,1)} %param.25) | copy-start | bytes 2064388
  0.6 34.0 %copy-start.6 = (s32[32]{0:T(128)S(1)}, s32[32]{0:T(128)}, u32[]{:S(2)}) copy-start(s32[32]{0:T(128)} %param.19) | copy-start | bytes 388
  30.9 8.9 %copy-start.2 = (bf16[2,2,3,64,768]{4,3,2,1,0:T(8,128)(2,1)S(1)}, bf16[2,2,3,64,768]{4,3,2,1,0:T(8,128)(2,1)}, u32[]{:S(2)}) copy-start(bf16[2,2,3,64,768]{4,3,2,1,0:T(8,128)(2,1)} %param.29) | copy-start | bytes 3538948
  30.9 20.3 %copy-start.3 = (f32[2,3,768]{2,0,1:T(2,128)S(1)}, f32[2,3,768]{2,0,1:T(2,128)}, u32[]{:S(2)}) copy-start(f32[2,3,768]{2,0,1:T(2,128)} %param.30) | copy-start | bytes 55300
  34.7 16.9 %copy-start.7 = (bf16[2,768,3,64]{1,3,2,0:T(8,128)(2,1)S(1)}, bf16[2,768,3,64]{1,3,2,0:T(8,128)(2,1)}, u32[]{:S(2)}) copy-start(bf16[2,768,3,64]{1,3,2,0:T(8,128)(2,1)} %param.27) | copy-start | bytes 1769476
  59.9 20.7 %copy-start.4 = (f32[2,768]{1,0:T(2,128)S(1)}, f32[2,768]{1,0:T(2,128)}, u32[]{:S(2)}) copy-start(f32[2,768]{1,0:T(2,128)} %param.32) | copy-start | bytes 18436
  94.6 22.9 %slice-start = ((s8[12582912]{0:T(1024)(128)(4,1)}), s8[4194304]{0:T(1024)(128)(4,1)S(1)}, s32[]{:S(2)}) async-start(s8[12582912]{0:T(1024)(128)(4,1)} %bitcast.235), calls=%async_computation | async-start | bytes 8388608
  96.6 22.2 %slice-start.3 = ((s8[12582912]{0:T(1024)(128)(4,1)}), s8[4194304]{0:T(1024)(128)(4,1)S(1)}, s32[]{:S(2)}) async-start(s8[12582912]{0:T(1024)(128)(4,1)} %bitcast.237), calls=%async_computation.3 | async-start | bytes 8388608
  96.7 20.7 %slice-start.1 = ((s8[12582912]{0:T(1024)(128)(4,1)}), s8[4194304]{0:T(1024)(128)(4,1)S(1)}, s32[]{:S(2)}) async-start(s8[12582912]{0:T(1024)(128)(4,1)} %bitcast.235), calls=%async_computation.1 | async-start | bytes 8388608
  96.7 20.7 %slice-start.2 = ((s8[12582912]{0:T(1024)(128)(4,1)}), s8[4194304]{0:T(1024)(128)(4,1)S(1)}, s32[]{:S(2)}) async-start(s8[12582912]{0:T(1024)(128)(4,1)} %bitcast.235), calls=%async_computation.2 | async-start | bytes 8388608
  96.8 22.1 %slice-start.4 = ((s8[12582912]{0:T(1024)(128)(4,1)}), s8[4194304]{0:T(1024)(128)(4,1)S(1)}, s32[]{:S(2)}) async-start(s8[12582912]{0:T(1024)(128)(4,1)} %bitcast.237), calls=%async_computation.4 | async-start | bytes 8388608
  96.8 23.0 %slice-start.5 = ((s8[12582912]{0:T(1024)(128)(4,1)}), s8[4194304]{0:T(1024)(128)(4,1)S(1)}, s32[]{:S(2)}) async-start(s8[12582912]{0:T(1024)(128)(4,1)} %bitcast.237), calls=%async_computation.5 | async-start | bytes 8388608
  150.7 25.8 %copy-start.5 = (f32[2,768]{1,0:T(2,128)S(1)}, f32[2,768]{1,0:T(2,128)}, u32[]{:S(2)}) copy-start(f32[2,768]{1,0:T(2,128)} %param.35) | copy-start | bytes 18436
  176.6 13.9 %copy-start.1 = (bf16[448,768]{1,0:T(8,128)(2,1)S(1)}, bf16[448,768]{1,0:T(8,128)(2,1)}, u32[]{:S(2)}) copy-start(bf16[448,768]{1,0:T(8,128)(2,1)} %param.25) | copy-start | bytes 2064388
where the time goes:
time: 191 us; the launch traced here: 190 us
  blocking collectives  81.2 us (43%)
  matrix products  67.8 us (35%)
  other arithmetic  27 us (14%)
  local copies, waits for them, and re-layouts  13.4 us (7%)
    psum x6, blocking collectives, group_sum(): return lax.psum(part_sum, 'tp').astype(jnp.bfloat16).astype(jnp.float32)  67.5 us
    select_n x1, other arithmetic, local_step(): jnp.where(write_mask, jnp.stack(new_val_rows)[:, :, None], self_vals)  20.6 us
    dot_general x2, matrix products, cross_attend(): jnp.einsum('bht,bthe->bhe', weights, val_rows, preferred_element_type=jnp...  17.8 us
    dot_general x2, matrix products, cross_attend(): jnp.einsum('bhe,bthe->bht', queries, key_rows, preferred_element_type=jnp...  15.4 us
    dot_general x1, matrix products, local_step(): jnp.einsum('bd,vd->bv', final_hidden, embed_table, preferred_element_type...  13.9 us
    psum x1, blocking collectives, local_step(): lax.psum(picked, 'tp').astype(jnp.float32)  13.6 us
    gather x1, local copies, waits for them, and re-layouts, local_step(): jnp.take(embed_table, jnp.clip(local_ids, 0, shard_rows - 1), axis=0)  9.94 us
    dot_general x2, matrix products, self_attend(): jnp.einsum('bht,bthe->bhe', past_weight, cache_vals, preferred_element_ty...  6.21 us

commit v1 on v0

v1 whole, which is shorter than its diff:
```python
import jax
import jax.numpy as jnp
from jax import lax
from jax.experimental import pallas as pl
from jax.experimental.pallas import tpu as pltpu
from jax.sharding import PartitionSpec as P

F32 = jnp.float32
BF16 = jnp.bfloat16
MESH = pl.DeviceIdType.MESH
ANY = pl.ANY

SLOTS = 19
UNROLL = 4
SELF_CHUNK = 8
VOCAB_CHUNK = 768
STAGE_SEQS = 4
STAGE_SLOTS = 8
MIB = 1024 * 1024


def layer_norm(residual, ln_gain, ln_shift):
    row_mean = jnp.mean(residual, axis=-1, keepdims=True)
    centred = residual - row_mean
    variance = jnp.mean(centred * centred, axis=-1, keepdims=True)
    return (centred * lax.rsqrt(variance + 1e-5) * ln_gain + ln_shift).astype(BF16)


def dot_nn(left, right):
    return lax.dot_general(left, right, (((1,), (0,)), ((), ())), preferred_element_type=F32)


def dot_nt(left, right):
    return lax.dot_general(left, right, (((1,), (1,)), ((), ())), preferred_element_type=F32)


def gather_kernel(tok_s, pos_s, embed_h, ptab_h, emb_o, pos_o, ebuf, pbuf, rows, esem, psem):
    n_seq = rows.shape[1]
    shard_rows = embed_h.shape[0]
    first = lax.axis_index('tp') * shard_rows

    def local_row(b):
        local = tok_s[b] - first
        owned = (local >= 0) & (local < shard_rows)
        return jnp.where(owned, local, 0), owned

    def e_copy(b):
        row, _ = local_row(b)
        base = pl.multiple_of((row // 16) * 16, 16)
        return pltpu.make_async_copy(embed_h.at[pl.ds(base, 16)], ebuf.at[b], esem.at[b])

    def p_copy(b):
        base = pl.multiple_of((pos_s[b] // 16) * 16, 16)
        return pltpu.make_async_copy(ptab_h.at[pl.ds(base, 16)], pbuf.at[b], psem.at[b])

    def start(b, carry):
        e_copy(b).start()
        p_copy(b).start()
        return carry

    lax.fori_loop(0, n_seq, start, 0)
    sub = lax.broadcasted_iota(jnp.int32, (16, embed_h.shape[1]), 0)

    def pick(b, carry):
        row, owned = local_row(b)
        e_copy(b).wait()
        p_copy(b).wait()
        want = jnp.where(owned, row % 16, -1)
        rows[0, pl.ds(b, 1), :] = jnp.sum(jnp.where(sub == want, ebuf[b].astype(F32), 0.0), axis=0, keepdims=True)
        rows[1, pl.ds(b, 1), :] = jnp.sum(jnp.where(sub == pos_s[b] % 16, pbuf[b].astype(F32), 0.0), axis=0, keepdims=True)
        return carry

    lax.fori_loop(0, n_seq, pick, 0)
    emb_o[...] = rows[0].astype(BF16)
    pos_o[...] = rows[1]


def layers_kernel(pos_s, picked, prow, inb, outb, lnp, bf1, lnf, wqkv_h, wcq_h, wout_h, w1_h, w2_h, sk_h, sv_h, ck_h, cv_h,
                  xo, kn, vn, skv,
                  x, q, o, ring, wqkv, wcq, wout, w1, w2, emb, ar, sem_w, sem_s, sem_c, sem_es, sem_er, sem_as, sem_ar):
    n_layer, n_seq, width = kn.shape
    half = n_seq // 2
    n_items = n_layer * n_seq
    n_chunk = n_seq // SELF_CHUNK
    me = lax.axis_index('tp')
    peers = [lax.rem(me + d, 4) for d in (1, 2, 3)]

    weights = ((wqkv_h, wqkv), (wcq_h, wcq), (wout_h, wout), (w1_h, w1), (w2_h, w2))

    def w_copy(i, layer):
        return pltpu.make_async_copy(weights[i][0].at[layer], weights[i][1].at[layer], sem_w.at[i, layer])

    def s_copy(kv, layer, c):
        rows = pl.ds(c * SELF_CHUNK, SELF_CHUNK)
        return pltpu.make_async_copy((sk_h, sv_h)[kv].at[layer, rows], skv.at[kv, layer, rows], sem_s.at[kv, layer, c])

    def c_copy(kv, item):
        slot = lax.rem(item, SLOTS)
        return pltpu.make_async_copy((ck_h, cv_h)[kv].at[lax.div(item, n_seq), lax.rem(item, n_seq)], ring.at[slot, kv], sem_c.at[kv, slot])

    def start_item(item):
        c_copy(0, item).start()
        c_copy(1, item).start()

    w_copy(0, 0).start()
    for c in range(n_chunk):
        s_copy(0, 0, c).start()
        s_copy(1, 0, c).start()
    w_copy(2, 0).start()
    w_copy(1, 0).start()
    for item in range(SLOTS):
        start_item(jnp.int32(item))
        if item == SLOTS // 2:
            w_copy(3, 0).start()
            w_copy(4, 0).start()
    for layer in range(1, n_layer):
        w_copy(0, layer).start()
        for c in range(n_chunk):
            s_copy(0, layer, c).start()
            s_copy(1, layer, c).start()
        for i in (2, 1, 3, 4):
            w_copy(i, layer).start()

    barrier = pltpu.get_barrier_semaphore()
    for peer in peers:
        pl.semaphore_signal(barrier, inc=1, device_id={'tp': peer}, device_id_type=MESH)
    pl.semaphore_wait(barrier, 3)

    def e_copy(d):
        return pltpu.make_async_remote_copy(picked, emb.at[me], sem_es.at[d], sem_er.at[d], device_id={'tp': peers[d]}, device_id_type=MESH)

    for d in range(3):
        e_copy(d).start()
    emb[me] = picked[...]
    for d in range(3):
        e_copy(d).wait()
    x[...] = (emb[0].astype(F32) + emb[1].astype(F32) + emb[2].astype(F32) + emb[3].astype(F32)) + prow[...]

    head_mask = lax.broadcasted_iota(jnp.int32, (8, width), 0) == lax.div(lax.broadcasted_iota(jnp.int32, (8, width), 1), 64)

    def a_copy(inst, d):
        return pltpu.make_async_remote_copy(ar.at[inst, me], ar.at[inst, me], sem_as.at[inst, d], sem_ar.at[inst, d], device_id={'tp': peers[d]}, device_id_type=MESH)

    def send(inst, part):
        ar[inst, me] = part
        for d in range(3):
            a_copy(inst, d).start()

    def receive(inst, rows, bias):
        for d in range(3):
            a_copy(inst, d).wait()
        total = (ar[inst, 0] + ar[inst, 1]) + (ar[inst, 2] + ar[inst, 3])
        x[rows, :] = (x[rows, :] + total.astype(BF16).astype(F32)) + bias

    def in_bias_row(kind, layer):
        return jnp.concatenate([inb[kind, h, pl.ds(layer, 1), :] for h in range(3)], axis=1)

    def query_block(b):
        return jnp.where(head_mask, q[pl.ds(b, 1), :] * 0.125, 0.0)

    def fold_heads(mixed):
        return jnp.sum(jnp.where(head_mask, mixed, 0.0), axis=0, keepdims=True)

    def self_stage(layer, hf):
        rows = pl.ds(hf * half, half)
        hidden = layer_norm(x[rows, :], lnp[layer, 0, 0:1, :], lnp[layer, 0, 1:2, :])
        if hf == 0:
            w_copy(0, layer).wait()
        round32 = lambda z: z.astype(BF16).astype(F32)
        q[rows, :] = round32(dot_nt(hidden, wqkv[layer, 0:width, :]) + in_bias_row(0, layer))
        kn[layer, rows, :] = round32(dot_nt(hidden, wqkv[layer, width:2 * width, :]))
        vn[layer, rows, :] = round32(dot_nt(hidden, wqkv[layer, 2 * width:3 * width, :]) + in_bias_row(1, layer))
        lane = lax.broadcasted_iota(jnp.int32, (8, skv.shape[4]), 1)

        def body(g, carry):
            seqs = [g * UNROLL + u for u in range(UNROLL)]
            blocks = [query_block(b) for b in seqs]
            scores = [dot_nn(blocks[u].astype(BF16), skv[0, layer, seqs[u]]) for u in range(UNROLL)]
            wts = []
            for u, b in enumerate(seqs):
                past = lane < pos_s[b]
                s = jnp.where(past, scores[u], -1e30)
                s_new = jnp.sum(blocks[u] * kn[layer, pl.ds(b, 1), :], axis=1, keepdims=True)
                peak = jnp.maximum(jnp.max(s, axis=1, keepdims=True), s_new)
                e = jnp.where(past, jnp.exp(s - peak), 0.0)
                e_new = jnp.exp(s_new - peak)
                inv = 1.0 / (jnp.sum(e, axis=1, keepdims=True) + e_new)
                wts.append(((e * inv).astype(BF16), (e_new * inv).astype(BF16).astype(F32)))
            for u, b in enumerate(seqs):
                mixed = dot_nt(wts[u][0], skv[1, layer, b]) + wts[u][1] * vn[layer, pl.ds(b, 1), :]
                o[pl.ds(b, 1), :] = fold_heads(mixed)
            return carry

        per = SELF_CHUNK // UNROLL
        for c in range(hf * half // SELF_CHUNK, (hf + 1) * half // SELF_CHUNK):
            s_copy(0, layer, c).wait()
            s_copy(1, layer, c).wait()
            lax.fori_loop(c * per, (c + 1) * per, body, 0)
        if hf == 0:
            w_copy(2, layer).wait()
        send((layer * 3 + 0) * 2 + hf, dot_nn(o[rows, :].astype(BF16), wout[layer, 0]))

    def cross_stage(layer, hf):
        rows = pl.ds(hf * half, half)
        hidden = layer_norm(x[rows, :], lnp[layer, 1, 0:1, :], lnp[layer, 1, 1:2, :])
        if hf == 0:
            w_copy(1, layer).wait()
        q[rows, :] = (dot_nt(hidden, wcq[layer]) + in_bias_row(2, layer)).astype(BF16).astype(F32)

        def body(g, carry):
            seqs = [g * UNROLL + u for u in range(UNROLL)]
            items = [layer * n_seq + b for b in seqs]
            slots = [lax.rem(item, SLOTS) for item in items]
            for item in items:
                c_copy(0, item).wait()
                c_copy(1, item).wait()
            scores = [dot_nn(query_block(seqs[u]).astype(BF16), ring[slots[u], 0]) for u in range(UNROLL)]
            wts = []
            for u in range(UNROLL):
                e = jnp.exp(scores[u] - jnp.max(scores[u], axis=1, keepdims=True))
                inv = 1.0 / jnp.sum(e, axis=1, keepdims=True)
                wts.append((e * inv).astype(BF16))
            for u, b in enumerate(seqs):
                o[pl.ds(b, 1), :] = fold_heads(dot_nt(wts[u], ring[slots[u], 1]))
            for item in items:
                @pl.when(item + SLOTS < n_items)
                def _():
                    start_item(item + SLOTS)
            return carry

        lax.fori_loop(hf * half // UNROLL, (hf + 1) * half // UNROLL, body, 0)
        send((layer * 3 + 1) * 2 + hf, dot_nn(o[rows, :].astype(BF16), wout[layer, 1]))

    def mlp_stage(layer, hf):
        rows = pl.ds(hf * half, half)
        hidden = layer_norm(x[rows, :], lnp[layer, 2, 0:1, :], lnp[layer, 2, 1:2, :])
        if hf == 0:
            w_copy(3, layer).wait()
            w_copy(4, layer).wait()
        pre = dot_nn(hidden, w1[layer]) + bf1[pl.ds(layer, 1), :]
        active = (0.5 * pre * (1.0 + lax.erf(pre * (0.5 ** 0.5)))).astype(BF16)
        send((layer * 3 + 2) * 2 + hf, dot_nn(active, w2[layer]))

    stages = (self_stage, cross_stage, mlp_stage)
    for step in range(n_layer * 3 + 1):
        layer, kind = divmod(step, 3)
        for hf in range(2):
            rows = pl.ds(hf * half, half)
            if step:
                prev_layer, prev_kind = divmod(step - 1, 3)
                receive((step - 1) * 2 + hf, rows, outb[prev_kind, prev_layer:prev_layer + 1, :])
            if step < n_layer * 3:
                stages[kind](layer, hf)
    xo[...] = layer_norm(x[...], lnf[0:1, :], lnf[1:2, :])


def tail_kernel(pos_s, xf, kn, vn, skv, embed_h, logit_h, nk_h, nv_h, ebuf, lbuf, stage, newt, sem_e, sem_l, sem_n):
    _, n_layer, n_seq, width, ctx = skv.shape
    n_vocab = ebuf.shape[0]
    n_chunk = n_seq // STAGE_SEQS

    def e_copy(c):
        return pltpu.make_async_copy(embed_h.at[pl.ds(pl.multiple_of(c * VOCAB_CHUNK, VOCAB_CHUNK), VOCAB_CHUNK)], ebuf.at[c], sem_e.at[c])

    def l_copy(c):
        return pltpu.make_async_copy(lbuf.at[c], logit_h.at[:, pl.ds(pl.multiple_of(c * VOCAB_CHUNK, VOCAB_CHUNK), VOCAB_CHUNK)], sem_l.at[c])

    for c in range(n_vocab):
        e_copy(c).start()

    lane = lax.broadcasted_iota(jnp.int32, (width, ctx), 1)
    col = lax.broadcasted_iota(jnp.int32, (width, n_seq), 1)

    for kv, (new, out_h) in enumerate(((kn, nk_h), (vn, nv_h))):
        for layer in range(n_layer):
            newt[...] = new[layer].T
            first = (kv * n_layer + layer) * n_chunk

            def n_copy(c, out_h=out_h, layer=layer, first=first):
                slot = lax.rem(c + first, STAGE_SLOTS)
                return pltpu.make_async_copy(stage.at[slot], out_h.at[layer, pl.ds(c * STAGE_SEQS, STAGE_SEQS)], sem_n.at[slot])

            def body(c, carry, kv=kv, layer=layer, first=first, n_copy=n_copy):
                @pl.when(c + first >= STAGE_SLOTS)
                def _():
                    n_copy(c).wait()
                slot = lax.rem(c + first, STAGE_SLOTS)
                for s in range(STAGE_SEQS):
                    b = c * STAGE_SEQS + s
                    column = jnp.sum(jnp.where(col == b, newt[...], 0.0), axis=1, keepdims=True)
                    stage[slot, s] = jnp.where(lane == pos_s[b], column, skv[kv, layer, b].astype(F32)).astype(BF16)
                n_copy(c).start()
                return carry

            lax.fori_loop(0, n_chunk, body, 0)

    def logit_body(c, carry):
        e_copy(c).wait()
        lbuf[c] = dot_nt(xf[...], ebuf[c])
        l_copy(c).start()
        return carry

    lax.fori_loop(0, n_vocab, logit_body, 0)

    def drain(c, carry):
        l_copy(c).wait()
        return carry

    lax.fori_loop(0, n_vocab, drain, 0)
    for slot in range(STAGE_SLOTS):
        pltpu.make_async_copy(stage.at[slot], nv_h.at[0, pl.ds(0, STAGE_SEQS)], sem_n.at[slot]).wait()


def solution(mesh):
    smem = pl.BlockSpec(memory_space=pltpu.SMEM)
    vmem = pl.BlockSpec(memory_space=pltpu.VMEM)
    hbm = pl.BlockSpec(memory_space=ANY)
    dma = pltpu.SemaphoreType.DMA
    on_chip = lambda z: pltpu.with_memory_space_constraint(z, pltpu.VMEM)

    def local_step(tokens, positions, self_keys, self_vals, cross_keys, cross_vals, embed_table, pos_table, w_qkv, w_cq, in_bias, w_out, out_bias, w_fc1, b_fc1, w_fc2, ln_layers, ln_final):
        n_layer, n_seq, ctx, n_head, head_dim = self_keys.shape
        frames = cross_keys.shape[2]
        width = n_head * head_dim
        model = embed_table.shape[1]
        hidden_units = w_fc1.shape[2]
        vocab_rows = embed_table.shape[0]
        n_vocab = vocab_rows // VOCAB_CHUNK
        flat = lambda cache: jnp.transpose(cache, (0, 1, 3, 4, 2)).reshape(n_layer, n_seq, width, cache.shape[2])
        sk, sv, ck, cv = flat(self_keys), flat(self_vals), flat(cross_keys), flat(cross_vals)

        picked, prow = pl.pallas_call(
            gather_kernel,
            out_shape=(pltpu.VMEM((n_seq, model), BF16), pltpu.VMEM((n_seq, model), F32)),
            in_specs=[smem, smem, hbm, hbm],
            out_specs=(vmem, vmem),
            scratch_shapes=[
                pltpu.VMEM((n_seq, 16, model), BF16), pltpu.VMEM((n_seq, 16, model), BF16), pltpu.VMEM((2, n_seq, model), F32),
                dma((n_seq,)), dma((n_seq,)),
            ],
            name='gather_rows',
        )(tokens, positions, embed_table, pos_table)

        wqkv = jnp.transpose(w_qkv, (0, 2, 3, 4, 1)).reshape(n_layer, 3 * width, model)
        wcq = jnp.transpose(w_cq, (0, 2, 3, 1)).reshape(n_layer, width, model)
        wout = w_out.reshape(n_layer, 2, width, model)
        n_inst = n_layer * 3 * 2
        xf, kn, vn, skv = pl.pallas_call(
            layers_kernel,
            out_shape=(
                pltpu.VMEM((n_seq, model), BF16),
                pltpu.VMEM((n_layer, n_seq, width), F32),
                pltpu.VMEM((n_layer, n_seq, width), F32),
                pltpu.VMEM((2,) + sk.shape, BF16),
            ),
            in_specs=[smem] + [vmem] * 7 + [hbm] * 9,
            out_specs=(vmem, vmem, vmem, vmem),
            scratch_shapes=[
                pltpu.VMEM((n_seq, model), F32), pltpu.VMEM((n_seq, width), F32), pltpu.VMEM((n_seq, width), F32),
                pltpu.VMEM((SLOTS, 2, width, frames), BF16),
                pltpu.VMEM(wqkv.shape, BF16), pltpu.VMEM(wcq.shape, BF16), pltpu.VMEM(wout.shape, BF16),
                pltpu.VMEM(w_fc1.shape, BF16), pltpu.VMEM(w_fc2.shape, BF16),
                pltpu.VMEM((4, n_seq, model), BF16), pltpu.VMEM((n_inst, 4, n_seq // 2, model), F32),
                dma((5, n_layer)), dma((2, n_layer, n_seq // SELF_CHUNK)), dma((2, SLOTS)), dma((3,)), dma((3,)), dma((n_inst, 3)), dma((n_inst, 3)),
            ],
            compiler_params=pltpu.CompilerParams(collective_id=0, has_side_effects=True, vmem_limit_bytes=37 * MIB),
            name='decoder_layers',
        )(positions, on_chip(picked), on_chip(prow), jnp.transpose(in_bias, (1, 2, 0, 3)), jnp.transpose(out_bias, (1, 0, 2)), ln_layers, b_fc1, ln_final,
          wqkv, wcq, wout, w_fc1, w_fc2, sk, sv, ck, cv)

        logits, nk, nv = pl.pallas_call(
            tail_kernel,
            out_shape=(
                jax.ShapeDtypeStruct((n_seq, vocab_rows), F32),
                jax.ShapeDtypeStruct(sk.shape, BF16),
                jax.ShapeDtypeStruct(sv.shape, BF16),
            ),
            in_specs=[smem, vmem, vmem, vmem, vmem, hbm],
            out_specs=(hbm, hbm, hbm),
            scratch_shapes=[
                pltpu.VMEM((n_vocab, VOCAB_CHUNK, model), BF16), pltpu.VMEM((n_vocab, n_seq, VOCAB_CHUNK), F32),
                pltpu.VMEM((STAGE_SLOTS, STAGE_SEQS, width, ctx), BF16), pltpu.VMEM((width, n_seq), F32),
                dma((n_vocab,)), dma((n_vocab,)), dma((STAGE_SLOTS,)),
            ],
            compiler_params=pltpu.CompilerParams(vmem_limit_bytes=34 * MIB),
            name='logits_and_caches',
        )(positions, *(on_chip(z) for z in (xf, kn, vn, skv)), embed_table)
        unflat = lambda cache: jnp.transpose(cache.reshape(n_layer, n_seq, n_head, head_dim, ctx), (0, 1, 4, 2, 3))
        return logits, unflat(nk), unflat(nv)

    batch_spec = P('dp')
    cache_spec = P(None, 'dp', None, 'tp', None)
    in_specs = (batch_spec, batch_spec, cache_spec, cache_spec, cache_spec, cache_spec, P('tp', None), P(None, None), P(None, None, None, 'tp', None), P(None, None, 'tp', None), P(None, None, 'tp', None), P(None, None, 'tp', None, None), P(None, None, None), P(None, None, 'tp'), P(None, 'tp'), P(None, 'tp', None), P(None, None, None, None), P(None, None))
    out_specs = (P('dp', 'tp'), cache_spec, cache_spec)
    return jax.shard_map(local_step, mesh=mesh, in_specs=in_specs, out_specs=out_specs, check_vma=False)
```

time: 191 us -> 85.2 us (0.45)
  Pallas kernels: 0 us -> 84.3 us
  blocking collectives: 81.2 us -> 0 us
  matrix products: 67.8 us -> 0 us
  other arithmetic: 27 us -> 0 us
  local copies, waits for them, and re-layouts: 13.4 us -> 0 us
    pallas_call x0 -> x3, Pallas kernels: none -> 84.3 us  [the longest x1 61.1 us: local_step(): pl.pallas_call(layers_kernel, out_shape=(pltpu.VMEM((n_seq, model), BF16)...]
    psum x7 -> x0, blocking collectives: 81.2 us -> none  [the longest x6 67.5 us: group_sum(): return lax.psum(part_sum, 'tp').astype(jnp.bfloat16).astype(jnp.float32)]
    dot_general x19 -> x0, matrix products: 67.8 us -> none  [the longest x2 17.8 us: cross_attend(): jnp.einsum('bht,bthe->bhe', weights, val_rows, preferred_element_type=jnp...]
    select_n x4 -> x0, other arithmetic: 21.4 us -> none  [the longest x1 20.6 us: local_step(): jnp.where(write_mask, jnp.stack(new_val_rows)[:, :, None], self_vals)]
    gather x2 -> x0, local copies, waits for them, and re-layouts: 10.6 us -> none  [the longest x1 9.94 us: local_step(): jnp.take(embed_table, jnp.clip(local_ids, 0, shard_rows - 1), axis=0)]
    reduce_sum x16 -> x0, other arithmetic: 2.71 us -> none  [the longest x7 1.33 us: layer_norm(): variance = jnp.mean(centred * centred, axis=-1, keepdims=True)]
where the time goes in v1:
time: 85.2 us; the launch traced here: 84.9 us
  Pallas kernels  84.3 us (99%)
    pallas_call x1, Pallas kernels, local_step(): pl.pallas_call(layers_kernel, out_shape=(pltpu.VMEM((n_seq, model), BF16)...  61.1 us
    pallas_call x1, Pallas kernels, local_step(): pl.pallas_call(tail_kernel, out_shape=(jax.ShapeDtypeStruct((n_seq, vocab...  19.7 us
    pallas_call x1, Pallas kernels, local_step(): pl.pallas_call(gather_kernel, out_shape=(pltpu.VMEM((n_seq, model), BF16)...  3.48 us

profile of v1, /device:TPU:0, one launch (start us, length us, event | category | flops | bytes accessed | tf_op | source)
XLA Modules:
  0.0 84.9 jit_solution(17377176949918506555)
XLA Ops:
  0.6 3.5 %gather_rows.1 = (bf16[32,768]{1,0:T(8,128)(2,1)S(1)}, f32[32,768]{1,0:T(8,128)S(1)}) custom-call(s32[32]{0:T(128)} %tok_s.1, s32[32]{0:T(128)} %pos_s.5, bf16[13056,768]{1,0:T(8,128)(2,1)} %embed_h.3, bf16[448,768]{1,0:T(8,128)(2,1)} %ptab_h.1), custom_call_target="tpu_custom_call" | custom-call | tf_op jit(solution)/shard_map/gather_rows/pallas_call | solution.py:332
  4.1 61.1 %decoder_layers.1 = (bf16[32,768]{1,0:T(8,128)(2,1)S(1)}, f32[2,32,192]{2,1,0:T(8,128)S(1)}, f32[2,32,192]{2,1,0:T(8,128)S(1)}, bf16[2,2,32,192,448]{4,3,2,1,0:T(8,128)(2,1)S(1)}) custom-call(s32[32]{0:T(128)} %pos_s.5, bf16[32,768]{1,0:T(8,128)(2,1)S(1)} %get-tuple-element.12.picked, f32[32,768]{1,0:T(8,128)S(1)} %get-tuple-element.13.prow, ...), custom_call_target="tpu_custom_call" | custom-call | tf_op jit(solution)/shard_map/decoder_layers/pallas_call | solution.py:348
  65.2 19.7 %logits_and_caches.1 = (f32[32,13056]{1,0:T(8,128)}, bf16[2,32,192,448]{3,2,1,0:T(8,128)(2,1)}, bf16[2,32,192,448]{3,2,1,0:T(8,128)(2,1)}) custom-call(s32[32]{0:T(128)} %pos_s.5, bf16[32,768]{1,0:T(8,128)(2,1)S(1)} %get-tuple-element.14.xf, f32[2,32,192]{2,1,0:T(8,128)S(1)} %get-tuple-element.15.kn, f32[2,32,192]{2,1,0:T(8,128)S(1)} %get-tuple-element.16.vn, ...), custom_call_target="tpu_custom_call" | custom-call | tf_op jit(solution)/shard_map/logits_and_caches/pallas_call | solution.py:371

commit v2 on v1

v2 whole, which is shorter than its diff:
```python
import jax
import jax.numpy as jnp
from jax import lax
from jax.experimental import pallas as pl
from jax.experimental.pallas import tpu as pltpu
from jax.sharding import PartitionSpec as P

F32 = jnp.float32
BF16 = jnp.bfloat16
MESH = pl.DeviceIdType.MESH
ANY = pl.ANY

SLOTS = 5
GROUP = 4
PARTS = 2
BLOCK = 2
VOCAB_AHEAD = 5
LOGIT_LAG = 2
VOCAB_CHUNK = 768
STAGE_SLOTS = 8
MIB = 1024 * 1024


def layer_norm(residual, ln_gain, ln_shift):
    row_mean = jnp.mean(residual, axis=-1, keepdims=True)
    centred = residual - row_mean
    variance = jnp.mean(centred * centred, axis=-1, keepdims=True)
    return (centred * lax.rsqrt(variance + 1e-5) * ln_gain + ln_shift).astype(BF16)


def dot_nn(left, right):
    return lax.dot_general(left, right, (((1,), (0,)), ((), ())), preferred_element_type=F32)


def dot_nt(left, right):
    return lax.dot_general(left, right, (((1,), (1,)), ((), ())), preferred_element_type=F32)


def gather_kernel(tok_s, embed_h, emb_o, ebuf, rows, esem):
    n_seq = rows.shape[0]
    shard_rows = embed_h.shape[0]
    first = lax.axis_index('tp') * shard_rows

    def local_row(b):
        local = tok_s[b] - first
        owned = (local >= 0) & (local < shard_rows)
        return jnp.where(owned, local, 0), owned

    def e_copy(b):
        row, _ = local_row(b)
        base = pl.multiple_of((row // 16) * 16, 16)
        return pltpu.make_async_copy(embed_h.at[pl.ds(base, 16)], ebuf.at[b], esem.at[b])

    for b in range(n_seq):
        e_copy(b).start()
    sub = lax.broadcasted_iota(jnp.int32, (16, embed_h.shape[1]), 0)
    for b in range(n_seq):
        row, owned = local_row(b)
        e_copy(b).wait()
        want = jnp.where(owned, row % 16, -1)
        rows[b:b + 1, :] = jnp.sum(jnp.where(sub == want, ebuf[b].astype(F32), 0.0), axis=0, keepdims=True)
    emb_o[...] = rows[...].astype(BF16)


def layers_kernel(pos_s, picked, inb, outb, lnp, bf1, lnf, ptab_h, wqkv_h, wcq_h, wout_h, w1_h, w2_h, sk_h, sv_h, ck_h, cv_h,
                  xo, kn, vn, skv,
                  x, of, hot, ptab, ring, wqkv, wcq, wout, w1, w2, emb, ar, sem_p, sem_w, sem_s, sem_c, sem_es, sem_er, sem_as, sem_ar):
    n_layer, n_seq, width = kn.shape
    per_part = n_seq // PARTS
    n_group = per_part // GROUP
    layer_items = PARTS * n_group
    n_items = n_layer * layer_items
    stacked = GROUP * width
    frames = ring.shape[-1]
    ctx = skv.shape[-1]
    me = lax.axis_index('tp')
    peers = [lax.rem(me + d, 4) for d in (1, 2, 3)]

    weights = ((wqkv_h, wqkv), (wcq_h, wcq), (wout_h, wout), (w1_h, w1), (w2_h, w2))

    def w_copy(i, layer):
        return pltpu.make_async_copy(weights[i][0].at[layer], weights[i][1].at[layer], sem_w.at[i, layer])

    def s_copy(kv, layer, item):
        part, g = divmod(item, n_group)
        return pltpu.make_async_copy((sk_h, sv_h)[kv].at[layer, part, :, g], skv.at[kv, layer, item], sem_s.at[kv, layer, item])

    def c_copy(kv, item):
        slot = item % SLOTS
        layer, rest = divmod(item, layer_items)
        part, g = divmod(rest, n_group)
        return pltpu.make_async_copy((ck_h, cv_h)[kv].at[layer, part, :, g], ring.at[kv, slot], sem_c.at[kv, slot])

    def start_self(layer, part):
        for item in range(part * n_group, (part + 1) * n_group):
            s_copy(0, layer, item).start()
            s_copy(1, layer, item).start()

    def start_weights(layer, which):
        for i in which:
            w_copy(i, layer).start()

    def start_cross(items):
        for item in items:
            if item < n_items:
                c_copy(0, item).start()
                c_copy(1, item).start()

    tab_copy = pltpu.make_async_copy(ptab_h, ptab, sem_p.at[0])
    tab_copy.start()
    start_weights(0, (0,))
    for part in range(PARTS):
        start_self(0, part)
        start_weights(0, ((2,), (1,))[part])

    barrier = pltpu.get_barrier_semaphore()
    for peer in peers:
        pl.semaphore_signal(barrier, inc=1, device_id={'tp': peer}, device_id_type=MESH)
    pl.semaphore_wait(barrier, 3)
    start_cross((0,))

    def e_copy(d):
        return pltpu.make_async_remote_copy(picked, emb.at[me], sem_es.at[d], sem_er.at[d], device_id={'tp': peers[d]}, device_id_type=MESH)

    for d in range(3):
        e_copy(d).start()
    emb[me] = picked[...]
    tab_lane = lax.broadcasted_iota(jnp.int32, (1, ptab.shape[0]), 1)
    for b in range(n_seq):
        hot[b:b + 1, :] = jnp.where(tab_lane == pos_s[b], 1.0, 0.0)
    tab_copy.wait()
    x[...] = dot_nn(hot[...].astype(BF16), ptab[...])
    for d in range(3):
        e_copy(d).wait()
    x[...] = (emb[0].astype(F32) + emb[1].astype(F32) + emb[2].astype(F32) + emb[3].astype(F32)) + x[...]
    start_cross((1, 2))

    lane_block = lax.div(lax.broadcasted_iota(jnp.int32, (16, stacked), 1), 64)
    block_mask = lax.broadcasted_iota(jnp.int32, (16, stacked), 0) == lane_block
    row_seq = lax.div(lax.broadcasted_iota(jnp.int32, (16, 1), 0), width // 64)
    lane = lax.broadcasted_iota(jnp.int32, (16, ctx), 1)

    def a_copy(inst, d):
        return pltpu.make_async_remote_copy(ar.at[inst, me], ar.at[inst, me], sem_as.at[inst, d], sem_ar.at[inst, d], device_id={'tp': peers[d]}, device_id_type=MESH)

    def send(inst, value):
        ar[inst, me] = value
        for d in range(3):
            a_copy(inst, d).start()

    def receive(inst, rows, bias):
        for d in range(3):
            a_copy(inst, d).wait()
        total = (ar[inst, 0] + ar[inst, 1]) + (ar[inst, 2] + ar[inst, 3])
        x[rows, :] = (x[rows, :] + total.astype(BF16).astype(F32)) + bias

    def in_bias_row(kind, layer):
        return jnp.concatenate([inb[kind, h, layer:layer + 1, :] for h in range(3)], axis=1)

    def stack(rows):
        return jnp.concatenate([rows[u * n_group:(u + 1) * n_group] for u in range(GROUP)], axis=1)

    def query_blocks(flat):
        return [jnp.where(block_mask, flat[g:g + 1] * 0.125, 0.0) for g in range(n_group)]

    def fold(mixed):
        return jnp.sum(jnp.where(block_mask, mixed, 0.0), axis=0, keepdims=True)

    def attended():
        return jnp.concatenate([of[:, u * width:(u + 1) * width] for u in range(GROUP)], axis=0).astype(BF16)

    def round32(z):
        return z.astype(BF16).astype(F32)

    def self_stage(layer, part, rows):
        hidden = layer_norm(x[rows, :], lnp[layer, 0, 0:1, :], lnp[layer, 0, 1:2, :])

        if part == 0:
            w_copy(0, layer).wait()
            w_copy(2, layer).wait()

        q = round32(dot_nt(hidden, wqkv[layer, 0:width, :]) + in_bias_row(0, layer))
        k_new = round32(dot_nt(hidden, wqkv[layer, width:2 * width, :]))
        v_new = round32(dot_nt(hidden, wqkv[layer, 2 * width:3 * width, :]) + in_bias_row(1, layer))
        kn[layer, rows, :] = k_new
        vn[layer, rows, :] = v_new
        k_flat, v_flat = stack(k_new), stack(v_new)
        items = [part * n_group + g for g in range(n_group)]
        for item in items:
            s_copy(0, layer, item).wait()
            s_copy(1, layer, item).wait()
        blocks = query_blocks(stack(q))
        scores = [dot_nn(blocks[g].astype(BF16), skv[0, layer, items[g]].reshape(stacked, ctx)) for g in range(n_group)]
        mixed = []
        for g in range(n_group):
            limit = jnp.full((16, 1), 0, jnp.int32)
            for u in range(GROUP):
                limit = jnp.where(row_seq == u, pos_s[part * per_part + u * n_group + g], limit)
            past = lane < limit
            s = jnp.where(past, scores[g], -1e30)
            s_new = jnp.sum(blocks[g] * k_flat[g:g + 1], axis=1, keepdims=True)
            peak = jnp.maximum(jnp.max(s, axis=1, keepdims=True), s_new)
            e = jnp.where(past, jnp.exp(s - peak), 0.0)
            e_new = jnp.exp(s_new - peak)
            inv = 1.0 / (jnp.sum(e, axis=1, keepdims=True) + e_new)
            w_new = round32(e_new * inv)
            mixed.append(dot_nt((e * inv).astype(BF16), skv[1, layer, items[g]].reshape(stacked, ctx)) + w_new * v_flat[g:g + 1])
        for g in range(n_group):
            of[g:g + 1, :] = fold(mixed[g])
        return dot_nn(attended(), wout[layer, 0])

    def cross_stage(layer, part, rows):
        hidden = layer_norm(x[rows, :], lnp[layer, 1, 0:1, :], lnp[layer, 1, 1:2, :])

        if part == 0:
            w_copy(1, layer).wait()

        q = round32(dot_nt(hidden, wcq[layer]) + in_bias_row(2, layer))
        blocks = query_blocks(stack(q))
        items = [(layer * PARTS + part) * n_group + g for g in range(n_group)]
        mixed = []
        for first in range(0, n_group, BLOCK):
            block = range(first, first + BLOCK)
            for g in block:
                c_copy(0, items[g]).wait()
                c_copy(1, items[g]).wait()
            scores = [dot_nn(blocks[g].astype(BF16), ring[0, items[g] % SLOTS].reshape(stacked, frames)) for g in block]
            for g in block:
                s = scores[g - first]
                e = jnp.exp(s - jnp.max(s, axis=1, keepdims=True))
                inv = 1.0 / jnp.sum(e, axis=1, keepdims=True)
                mixed.append(dot_nt((e * inv).astype(BF16), ring[1, items[g] % SLOTS].reshape(stacked, frames)))
            for g in block:
                of[g:g + 1, :] = fold(mixed[g])
            start_cross([items[g] + SLOTS for g in block])
        heads = attended()
        return dot_nn(heads, wout[layer, 1])

    def mlp_stage(layer, part, rows):
        hidden = layer_norm(x[rows, :], lnp[layer, 2, 0:1, :], lnp[layer, 2, 1:2, :])

        if part == 0:
            w_copy(3, layer).wait()
            w_copy(4, layer).wait()

        pre = dot_nn(hidden, w1[layer]) + bf1[layer:layer + 1, :]
        active = (0.5 * pre * (1.0 + lax.erf(pre * (0.5 ** 0.5)))).astype(BF16)
        return dot_nn(active, w2[layer])

    stages = (self_stage, cross_stage, mlp_stage)
    def start_ahead(layer, kind, part):
        if kind == 0 and layer == 0:
            if part == 0:
                start_cross((3,))
            else:
                start_cross((4,))
                start_weights(0, (3, 4))
        if layer + 1 < n_layer:
            if kind == 1:
                if part == 0:
                    start_weights(layer + 1, (0,))
                start_self(layer + 1, part)
                start_weights(layer + 1, ((2,), (1,))[part])
            if kind == 2 and part == 0:
                start_weights(layer + 1, (3, 4))

    for step in range(n_layer * 3 + 1):
        for part in range(PARTS):
            rows = pl.ds(part * per_part, per_part)
            if step:
                prev_layer, prev_kind = divmod(step - 1, 3)
                receive((step - 1) * PARTS + part, rows, outb[prev_kind, prev_layer:prev_layer + 1, :])
            if step < n_layer * 3:
                layer, kind = divmod(step, 3)
                send(step * PARTS + part, stages[kind](layer, part, rows))
                start_ahead(layer, kind, part)
    xo[...] = layer_norm(x[...], lnf[0:1, :], lnf[1:2, :])


def tail_kernel(pos_s, xf, kn, vn, skv, embed_h, logit_h, nk_h, nv_h, ebuf, lbuf, stage, newt, sem_e, sem_l, sem_n):
    _, n_layer, n_chunk, _, width, ctx = skv.shape
    n_seq = n_chunk * GROUP
    n_group = n_chunk // PARTS
    n_vocab = lbuf.shape[0]
    n_write = 2 * n_layer * n_chunk

    def e_copy(c):
        return pltpu.make_async_copy(embed_h.at[pl.ds(c * VOCAB_CHUNK, VOCAB_CHUNK)], ebuf.at[c], sem_e.at[c])

    def l_copy(c):
        return pltpu.make_async_copy(lbuf.at[c], logit_h.at[:, pl.ds(c * VOCAB_CHUNK, VOCAB_CHUNK)], sem_l.at[c])

    def n_copy(i):
        kv, layer, c = i // (n_layer * n_chunk), i // n_chunk % n_layer, i % n_chunk
        return pltpu.make_async_copy(stage.at[i % STAGE_SLOTS], (nk_h, nv_h)[kv].at[layer, c // n_group, :, c % n_group], sem_n.at[i % STAGE_SLOTS])

    lane = lax.broadcasted_iota(jnp.int32, (16, ctx), 1)

    def write(i):
        kv, layer, c = i // (n_layer * n_chunk), i // n_chunk % n_layer, i % n_chunk
        if c == 0:
            newt[...] = (kn, vn)[kv][layer].T
        if i >= STAGE_SLOTS:
            n_copy(i - STAGE_SLOTS).wait()
        for s in range(GROUP):
            b = (c // n_group * GROUP + s) * n_group + c % n_group
            here = lane == pos_s[b]
            for r in range(0, width, 16):
                column = jnp.broadcast_to(newt[r:r + 16, b:b + 1], (16, ctx)).astype(BF16)
                stage[i % STAGE_SLOTS, s, r:r + 16, :] = jnp.where(here, column, skv[kv, layer, c, s, r:r + 16, :])
        n_copy(i).start()

    def logit(c):
        e_copy(c).wait()
        lbuf[c] = dot_nt(xf[...], ebuf[c])
        l_copy(c).start()

    done = 0
    for c in range(VOCAB_AHEAD):
        e_copy(c).start()
    for i in range(n_write):
        write(i)
        if i % 2 and i // 2 + VOCAB_AHEAD < n_vocab:
            e_copy(i // 2 + VOCAB_AHEAD).start()
        if i >= LOGIT_LAG and i % 2 == 0:
            logit(done)
            done += 1
    for c in range(done, n_vocab):
        logit(c)
    for c in range(n_vocab):
        l_copy(c).wait()
    for i in range(n_write - STAGE_SLOTS, n_write):
        n_copy(i).wait()


def solution(mesh):
    smem = pl.BlockSpec(memory_space=pltpu.SMEM)
    vmem = pl.BlockSpec(memory_space=pltpu.VMEM)
    hbm = pl.BlockSpec(memory_space=ANY)
    dma = pltpu.SemaphoreType.DMA
    on_chip = lambda z: pltpu.with_memory_space_constraint(z, pltpu.VMEM)

    def local_step(tokens, positions, self_keys, self_vals, cross_keys, cross_vals, embed_table, pos_table, w_qkv, w_cq, in_bias, w_out, out_bias, w_fc1, b_fc1, w_fc2, ln_layers, ln_final):
        n_layer, n_seq, ctx, n_head, head_dim = self_keys.shape
        frames = cross_keys.shape[2]
        width = n_head * head_dim
        model = embed_table.shape[1]
        hidden_units = w_fc1.shape[2]
        vocab_rows = embed_table.shape[0]
        n_vocab = vocab_rows // VOCAB_CHUNK
        n_group = n_seq // (PARTS * GROUP)
        flat = lambda cache: jnp.transpose(cache, (0, 1, 3, 4, 2)).reshape(n_layer, PARTS, GROUP, n_group, width, cache.shape[2])
        sk, sv, ck, cv = flat(self_keys), flat(self_vals), flat(cross_keys), flat(cross_vals)

        picked = pl.pallas_call(
            gather_kernel,
            out_shape=pltpu.VMEM((n_seq, model), BF16),
            in_specs=[smem, hbm],
            out_specs=vmem,
            scratch_shapes=[pltpu.VMEM((n_seq, 16, model), BF16), pltpu.VMEM((n_seq, model), F32), dma((n_seq,))],
            name='gather_rows',
        )(tokens, embed_table)

        wqkv = jnp.transpose(w_qkv, (0, 2, 3, 4, 1)).reshape(n_layer, 3 * width, model)
        wcq = jnp.transpose(w_cq, (0, 2, 3, 1)).reshape(n_layer, width, model)
        wout = w_out.reshape(n_layer, 2, width, model)
        n_inst = n_layer * 3 * PARTS
        n_item = PARTS * n_group
        xf, kn, vn, skv = pl.pallas_call(
            layers_kernel,
            out_shape=(
                pltpu.VMEM((n_seq, model), BF16),
                pltpu.VMEM((n_layer, n_seq, width), F32),
                pltpu.VMEM((n_layer, n_seq, width), F32),
                pltpu.VMEM((2, n_layer, n_item, GROUP, width, ctx), BF16),
            ),
            in_specs=[smem] + [vmem] * 6 + [hbm] * 10,
            out_specs=(vmem, vmem, vmem, vmem),
            scratch_shapes=[
                pltpu.VMEM((n_seq, model), F32), pltpu.VMEM((n_group, GROUP * width), F32),
                pltpu.VMEM((n_seq, ctx), F32), pltpu.VMEM(pos_table.shape, BF16),
                pltpu.VMEM((2, SLOTS, GROUP, width, frames), BF16),
                pltpu.VMEM(wqkv.shape, BF16), pltpu.VMEM(wcq.shape, BF16), pltpu.VMEM(wout.shape, BF16),
                pltpu.VMEM(w_fc1.shape, BF16), pltpu.VMEM(w_fc2.shape, BF16),
                pltpu.VMEM((4, n_seq, model), BF16), pltpu.VMEM((n_inst, 4, n_seq // PARTS, model), F32),
                dma((1,)), dma((5, n_layer)), dma((2, n_layer, n_item)), dma((2, SLOTS)), dma((3,)), dma((3,)), dma((n_inst, 3)), dma((n_inst, 3)),
            ],
            compiler_params=pltpu.CompilerParams(collective_id=0, has_side_effects=True, vmem_limit_bytes=37 * MIB),
            name='decoder_layers',
        )(positions, on_chip(picked), jnp.transpose(in_bias, (1, 2, 0, 3)), jnp.transpose(out_bias, (1, 0, 2)), ln_layers, b_fc1, ln_final,
          pos_table, wqkv, wcq, wout, w_fc1, w_fc2, sk, sv, ck, cv)

        logits, nk, nv = pl.pallas_call(
            tail_kernel,
            out_shape=(
                jax.ShapeDtypeStruct((n_seq, vocab_rows), F32),
                jax.ShapeDtypeStruct(sk.shape, BF16),
                jax.ShapeDtypeStruct(sv.shape, BF16),
            ),
            in_specs=[smem, vmem, vmem, vmem, vmem, hbm],
            out_specs=(hbm, hbm, hbm),
            scratch_shapes=[
                pltpu.VMEM((n_vocab, VOCAB_CHUNK, model), BF16), pltpu.VMEM((n_vocab, n_seq, VOCAB_CHUNK), F32),
                pltpu.VMEM((STAGE_SLOTS, GROUP, width, ctx), BF16), pltpu.VMEM((width, n_seq), F32),
                dma((n_vocab,)), dma((n_vocab,)), dma((STAGE_SLOTS,)),
            ],
            compiler_params=pltpu.CompilerParams(vmem_limit_bytes=34 * MIB),
            name='logits_and_caches',
        )(positions, *(on_chip(z) for z in (xf, kn, vn, skv)), embed_table)
        unflat = lambda cache: jnp.transpose(cache.reshape(n_layer, n_seq, n_head, head_dim, ctx), (0, 1, 4, 2, 3))
        return logits, unflat(nk), unflat(nv)

    batch_spec = P('dp')
    cache_spec = P(None, 'dp', None, 'tp', None)
    in_specs = (batch_spec, batch_spec, cache_spec, cache_spec, cache_spec, cache_spec, P('tp', None), P(None, None), P(None, None, None, 'tp', None), P(None, None, 'tp', None), P(None, None, 'tp', None), P(None, None, 'tp', None, None), P(None, None, None), P(None, None, 'tp'), P(None, 'tp'), P(None, 'tp', None), P(None, None, None, None), P(None, None))
    out_specs = (P('dp', 'tp'), cache_spec, cache_spec)
    return jax.shard_map(local_step, mesh=mesh, in_specs=in_specs, out_specs=out_specs, check_vma=False)
```

time: 85.2 us -> 77.7 us (0.912)
  Pallas kernels: 84.3 us -> 76.5 us
    pallas_call x1, Pallas kernels: 61.1 us -> 55.9 us  [local_step(): pl.pallas_call(layers_kernel, out_shape=(pltpu.VMEM((n_seq, model), BF16)...]
    pallas_call x1, Pallas kernels: 19.7 us -> 18 us  [local_step(): pl.pallas_call(tail_kernel, out_shape=(jax.ShapeDtypeStruct((n_seq, vocab...]
    pallas_call x1, Pallas kernels: 3.48 us -> 2.61 us  [local_step(): pl.pallas_call(gather_kernel, out_shape=pltpu.VMEM((n_seq, model), BF16),...]
where the time goes in v2:
time: 77.7 us; the launch traced here: 77.3 us
  Pallas kernels  76.5 us (98%)
  between operations  0.81 us (1%)
    pallas_call x1, Pallas kernels, local_step(): pl.pallas_call(layers_kernel, out_shape=(pltpu.VMEM((n_seq, model), BF16)...  55.9 us
    pallas_call x1, Pallas kernels, local_step(): pl.pallas_call(tail_kernel, out_shape=(jax.ShapeDtypeStruct((n_seq, vocab...  18 us
    pallas_call x1, Pallas kernels, local_step(): pl.pallas_call(gather_kernel, out_shape=pltpu.VMEM((n_seq, model), BF16),...  2.61 us

profile of v2, /device:TPU:0, one launch (start us, length us, event | category | flops | bytes accessed | tf_op | source)
XLA Modules:
  0.0 77.3 jit_solution(15922912273717719614)
XLA Ops:
  0.6 2.6 %gather_rows.1.picked = bf16[32,768]{1,0:T(8,128)(2,1)S(1)} custom-call(s32[32]{0:T(128)} %tok_s.1, bf16[13056,768]{1,0:T(8,128)(2,1)} %embed_h.3), custom_call_target="tpu_custom_call" | custom-call | tf_op jit(solution)/shard_map/gather_rows/pallas_call | solution.py:355
  3.3 55.9 %decoder_layers.1 = (bf16[32,768]{1,0:T(8,128)(2,1)S(1)}, f32[2,32,192]{2,1,0:T(8,128)S(1)}, f32[2,32,192]{2,1,0:T(8,128)S(1)}, bf16[2,2,8,4,192,448]{5,4,3,2,1,0:T(8,128)(2,1)S(1)}) custom-call(s32[32]{0:T(128)} %pos_s.3, bf16[32,768]{1,0:T(8,128)(2,1)S(1)} %gather_rows.1.picked, f32[3,3,2,64]{3,2,1,0:T(2,128)} %bitcast.35, f32[3,2,768]{2,1,0:T(2,128)} %bitcast.34, ...), custom_call_target="tpu_custom_call" | custom-call | tf_op jit(solution)/shard_map/decoder_layers/pallas_call | solution.py:369
  59.1 18.0 %logits_and_caches.1 = (f32[32,13056]{1,0:T(8,128)}, bf16[2,2,4,4,192,448]{5,4,3,2,1,0:T(8,128)(2,1)}, bf16[2,2,4,4,192,448]{5,4,3,2,1,0:T(8,128)(2,1)}) custom-call(s32[32]{0:T(128)} %pos_s.3, bf16[32,768]{1,0:T(8,128)(2,1)S(1)} %get-tuple-element.10.xf, f32[2,32,192]{2,1,0:T(8,128)S(1)} %get-tuple-element.11.kn, f32[2,32,192]{2,1,0:T(8,128)S(1)} %get-tuple-element.12.vn, ...), custom_call_target="tpu_custom_call" | custom-call | tf_op jit(solution)/shard_map/logits_and_caches/pallas_call | solution.py:393

commit v3 on v2

--- a/solution.py
+++ b/solution.py
@@ -14,8 +14,6 @@
 GROUP = 4
 PARTS = 2
 BLOCK = 2
-VOCAB_AHEAD = 5
-LOGIT_LAG = 2
 VOCAB_CHUNK = 768
 STAGE_SLOTS = 8
 MIB = 1024 * 1024
@@ -34,6 +32,10 @@
 
 def dot_nt(left, right):
     return lax.dot_general(left, right, (((1,), (1,)), ((), ())), preferred_element_type=F32)
+
+
+def chunk_place(c, n_items):
+    return c % 2, (n_items + c // 2 % SLOTS) % SLOTS
 
 
 def gather_kernel(tok_s, embed_h, emb_o, ebuf, rows, esem):
@@ -62,9 +64,9 @@
     emb_o[...] = rows[...].astype(BF16)
 
 
-def layers_kernel(pos_s, picked, inb, outb, lnp, bf1, lnf, ptab_h, wqkv_h, wcq_h, wout_h, w1_h, w2_h, sk_h, sv_h, ck_h, cv_h,
-                  xo, kn, vn, skv,
-                  x, of, hot, ptab, ring, wqkv, wcq, wout, w1, w2, emb, ar, sem_p, sem_w, sem_s, sem_c, sem_es, sem_er, sem_as, sem_ar):
+def layers_kernel(pos_s, picked, inb, outb, lnp, bf1, lnf, ptab_h, wqkv_h, wcq_h, wout_h, w1_h, w2_h, sk_h, sv_h, ck_h, cv_h, embed_h,
+                  xo, kn, vn, ext, ring, skv,
+                  x, of, hot, ptab, wqkv, wcq, wout, w1, w2, emb, ar, sem_p, sem_w, sem_s, sem_c, sem_v, sem_es, sem_er, sem_as, sem_ar):
     n_layer, n_seq, width = kn.shape
     per_part = n_seq // PARTS
     n_group = per_part // GROUP
@@ -100,11 +102,31 @@
         for i in which:
             w_copy(i, layer).start()
 
+    ahead = 2 * SLOTS
+    n_extra = ext.shape[0]
+    model = embed_h.shape[3]
+    split = model - ext.shape[3]
+
+    def v_copies(c):
+        kv, slot = chunk_place(c, n_items)
+        if c < ahead:
+            return [pltpu.make_async_copy(embed_h.at[c], ring.at[kv, slot, :, :, pl.ds(0, model)], sem_v.at[c])]
+        return [
+            pltpu.make_async_copy(embed_h.at[c, :, :, pl.ds(0, split)], ring.at[kv, slot, :, :, pl.ds(model, split)], sem_v.at[c]),
+            pltpu.make_async_copy(embed_h.at[c, :, :, pl.ds(split, model - split)], ext.at[c - ahead], sem_v.at[c + n_extra]),
+        ]
+
     def start_cross(items):
         for item in items:
-            if item < n_items:
-                c_copy(0, item).start()
-                c_copy(1, item).start()
+            for kv in range(2):
+                if item < n_items:
+                    c_copy(kv, item).start()
+                else:
+                    c = (item - n_items) * 2 + kv
+                    for chunk in (c, c + ahead):
+                        if chunk < ahead + n_extra:
+                            for copy in v_copies(chunk):
+                                copy.start()
 
     tab_copy = pltpu.make_async_copy(ptab_h, ptab, sem_p.at[0])
     tab_copy.start()
@@ -117,7 +139,7 @@
     for peer in peers:
         pl.semaphore_signal(barrier, inc=1, device_id={'tp': peer}, device_id_type=MESH)
     pl.semaphore_wait(barrier, 3)
-    start_cross((0,))
+    start_cross((0, 1))
 
     def e_copy(d):
         return pltpu.make_async_remote_copy(picked, emb.at[me], sem_es.at[d], sem_er.at[d], device_id={'tp': peers[d]}, device_id_type=MESH)
@@ -133,7 +155,7 @@
     for d in range(3):
         e_copy(d).wait()
     x[...] = (emb[0].astype(F32) + emb[1].astype(F32) + emb[2].astype(F32) + emb[3].astype(F32)) + x[...]
-    start_cross((1, 2))
+    start_cross((2, 3, 4))
 
     lane_block = lax.div(lax.broadcasted_iota(jnp.int32, (16, stacked), 1), 64)
     block_mask = lax.broadcasted_iota(jnp.int32, (16, stacked), 0) == lane_block
@@ -150,7 +172,7 @@
 
     def receive(inst, rows, bias):
         for d in range(3):
-            a_copy(inst, d).wait()
+            a_copy(inst, d).wait_recv()
         total = (ar[inst, 0] + ar[inst, 1]) + (ar[inst, 2] + ar[inst, 3])
         x[rows, :] = (x[rows, :] + total.astype(BF16).astype(F32)) + bias
 
@@ -250,10 +272,7 @@
     stages = (self_stage, cross_stage, mlp_stage)
     def start_ahead(layer, kind, part):
         if kind == 0 and layer == 0:
-            if part == 0:
-                start_cross((3,))
-            else:
-                start_cross((4,))
+            if part:
                 start_weights(0, (3, 4))
         if layer + 1 < n_layer:
             if kind == 1:
@@ -275,17 +294,23 @@
                 send(step * PARTS + part, stages[kind](layer, part, rows))
                 start_ahead(layer, kind, part)
     xo[...] = layer_norm(x[...], lnf[0:1, :], lnf[1:2, :])
-
-
-def tail_kernel(pos_s, xf, kn, vn, skv, embed_h, logit_h, nk_h, nv_h, ebuf, lbuf, stage, newt, sem_e, sem_l, sem_n):
+    for inst in range(n_layer * 3 * PARTS):
+        for d in range(3):
+            a_copy(inst, d).wait_send()
+    for c in range(ahead + n_extra):
+        for copy in v_copies(c):
+            copy.wait()
+
+
+def tail_kernel(pos_s, xf, kn, vn, ext, ring, skv, logit_h, nk_h, nv_h, lbuf, stage, newt, sem_l, sem_n):
     _, n_layer, n_chunk, _, width, ctx = skv.shape
     n_seq = n_chunk * GROUP
     n_group = n_chunk // PARTS
     n_vocab = lbuf.shape[0]
+    ahead = 2 * SLOTS
+    model = xf.shape[1]
+    split = model - ext.shape[3]
     n_write = 2 * n_layer * n_chunk
-
-    def e_copy(c):
-        return pltpu.make_async_copy(embed_h.at[pl.ds(c * VOCAB_CHUNK, VOCAB_CHUNK)], ebuf.at[c], sem_e.at[c])
 
     def l_copy(c):
         return pltpu.make_async_copy(lbuf.at[c], logit_h.at[:, pl.ds(c * VOCAB_CHUNK, VOCAB_CHUNK)], sem_l.at[c])
@@ -311,21 +336,22 @@
         n_copy(i).start()
 
     def logit(c):
-        e_copy(c).wait()
-        lbuf[c] = dot_nt(xf[...], ebuf[c])
+        kv, slot = chunk_place(c, n_layer * n_chunk)
+        if c < ahead:
+            lbuf[c] = dot_nt(xf[...], ring[kv, slot, :, :, 0:model].reshape(VOCAB_CHUNK, model))
+        else:
+            left = ring[kv, slot, :, :, model:model + split].reshape(VOCAB_CHUNK, split)
+            right = ext[c - ahead].reshape(VOCAB_CHUNK, model - split)
+            lbuf[c] = dot_nt(xf[:, 0:split], left) + dot_nt(xf[:, split:model], right)
         l_copy(c).start()
 
-    done = 0
-    for c in range(VOCAB_AHEAD):
-        e_copy(c).start()
-    for i in range(n_write):
+    for i in range(STAGE_SLOTS // 2):
         write(i)
-        if i % 2 and i // 2 + VOCAB_AHEAD < n_vocab:
-            e_copy(i // 2 + VOCAB_AHEAD).start()
-        if i >= LOGIT_LAG and i % 2 == 0:
-            logit(done)
-            done += 1
-    for c in range(done, n_vocab):
+    for i in range(STAGE_SLOTS // 2, n_write):
+        write(i)
+        if i % 2 and i // 2 < n_vocab:
+            logit(i // 2 - STAGE_SLOTS // 4)
+    for c in range(n_write // 2 - STAGE_SLOTS // 4, n_vocab):
         logit(c)
     for c in range(n_vocab):
         l_copy(c).wait()
@@ -364,31 +390,33 @@
         wqkv = jnp.transpose(w_qkv, (0, 2, 3, 4, 1)).reshape(n_layer, 3 * width, model)
         wcq = jnp.transpose(w_cq, (0, 2, 3, 1)).reshape(n_layer, width, model)
         wout = w_out.reshape(n_layer, 2, width, model)
+        embed_chunks = embed_table.reshape(n_vocab, GROUP, width, model)
         n_inst = n_layer * 3 * PARTS
         n_item = PARTS * n_group
-        xf, kn, vn, skv = pl.pallas_call(
+        xf, kn, vn, ext, ring, skv = pl.pallas_call(
             layers_kernel,
             out_shape=(
                 pltpu.VMEM((n_seq, model), BF16),
                 pltpu.VMEM((n_layer, n_seq, width), F32),
                 pltpu.VMEM((n_layer, n_seq, width), F32),
+                pltpu.VMEM((n_vocab - 2 * SLOTS, GROUP, width, 128), BF16),
+                pltpu.VMEM((2, SLOTS, GROUP, width, frames), BF16),
                 pltpu.VMEM((2, n_layer, n_item, GROUP, width, ctx), BF16),
             ),
-            in_specs=[smem] + [vmem] * 6 + [hbm] * 10,
-            out_specs=(vmem, vmem, vmem, vmem),
+            in_specs=[smem] + [vmem] * 6 + [hbm] * 11,
+            out_specs=(vmem,) * 6,
             scratch_shapes=[
                 pltpu.VMEM((n_seq, model), F32), pltpu.VMEM((n_group, GROUP * width), F32),
                 pltpu.VMEM((n_seq, ctx), F32), pltpu.VMEM(pos_table.shape, BF16),
-                pltpu.VMEM((2, SLOTS, GROUP, width, frames), BF16),
                 pltpu.VMEM(wqkv.shape, BF16), pltpu.VMEM(wcq.shape, BF16), pltpu.VMEM(wout.shape, BF16),
                 pltpu.VMEM(w_fc1.shape, BF16), pltpu.VMEM(w_fc2.shape, BF16),
                 pltpu.VMEM((4, n_seq, model), BF16), pltpu.VMEM((n_inst, 4, n_seq // PARTS, model), F32),
-                dma((1,)), dma((5, n_layer)), dma((2, n_layer, n_item)), dma((2, SLOTS)), dma((3,)), dma((3,)), dma((n_inst, 3)), dma((n_inst, 3)),
+                dma((1,)), dma((5, n_layer)), dma((2, n_layer, n_item)), dma((2, SLOTS)), dma((2 * n_vocab - 2 * SLOTS,)), dma((3,)), dma((3,)), dma((n_inst, 3)), dma((n_inst, 3)),
             ],
-            compiler_params=pltpu.CompilerParams(collective_id=0, has_side_effects=True, vmem_limit_bytes=37 * MIB),
+            compiler_params=pltpu.CompilerParams(collective_id=0, has_side_effects=True, vmem_limit_bytes=15 * MIB),
             name='decoder_layers',
         )(positions, on_chip(picked), jnp.transpose(in_bias, (1, 2, 0, 3)), jnp.transpose(out_bias, (1, 0, 2)), ln_layers, b_fc1, ln_final,
-          pos_table, wqkv, wcq, wout, w_fc1, w_fc2, sk, sv, ck, cv)
+          pos_table, wqkv, wcq, wout, w_fc1, w_fc2, sk, sv, ck, cv, embed_chunks)
 
         logits, nk, nv = pl.pallas_call(
             tail_kernel,
@@ -397,16 +425,16 @@
                 jax.ShapeDtypeStruct(sk.shape, BF16),
                 jax.ShapeDtypeStruct(sv.shape, BF16),
             ),
-            in_specs=[smem, vmem, vmem, vmem, vmem, hbm],
+            in_specs=[smem] + [vmem] * 6,
             out_specs=(hbm, hbm, hbm),
             scratch_shapes=[
-                pltpu.VMEM((n_vocab, VOCAB_CHUNK, model), BF16), pltpu.VMEM((n_vocab, n_seq, VOCAB_CHUNK), F32),
+                pltpu.VMEM((n_vocab, n_seq, VOCAB_CHUNK), F32),
                 pltpu.VMEM((STAGE_SLOTS, GROUP, width, ctx), BF16), pltpu.VMEM((width, n_seq), F32),
-                dma((n_vocab,)), dma((n_vocab,)), dma((STAGE_SLOTS,)),
+                dma((n_vocab,)), dma((STAGE_SLOTS,)),
             ],
-            compiler_params=pltpu.CompilerParams(vmem_limit_bytes=34 * MIB),
+            compiler_params=pltpu.CompilerParams(vmem_limit_bytes=15 * MIB),
             name='logits_and_caches',
-        )(positions, *(on_chip(z) for z in (xf, kn, vn, skv)), embed_table)
+        )(positions, *(on_chip(z) for z in (xf, kn, vn, ext, ring, skv)))
         unflat = lambda cache: jnp.transpose(cache.reshape(n_layer, n_seq, n_head, head_dim, ctx), (0, 1, 4, 2, 3))
         return logits, unflat(nk), unflat(nv)
 

time: 77.7 us -> 73 us (0.940)
  Pallas kernels: 76.5 us -> 72.1 us
    pallas_call x1, Pallas kernels: 18 us -> 12.8 us  [local_step(): pl.pallas_call(tail_kernel, out_shape=(jax.ShapeDtypeStruct((n_seq, vocab...]
    pallas_call x1, Pallas kernels: 55.9 us -> 56.7 us  [local_step(): pl.pallas_call(layers_kernel, out_shape=(pltpu.VMEM((n_seq, model), BF16)...]
where the time goes in v3:
time: 73 us; the launch traced here: 72.9 us
  Pallas kernels  72.1 us (99%)
  between operations  0.81 us (1%)
    pallas_call x1, Pallas kernels, local_step(): pl.pallas_call(layers_kernel, out_shape=(pltpu.VMEM((n_seq, model), BF16)...  56.7 us
    pallas_call x1, Pallas kernels, local_step(): pl.pallas_call(tail_kernel, out_shape=(jax.ShapeDtypeStruct((n_seq, vocab...  12.8 us
    pallas_call x1, Pallas kernels, local_step(): pl.pallas_call(gather_kernel, out_shape=pltpu.VMEM((n_seq, model), BF16),...  2.55 us

profile of v3, /device:TPU:0, one launch (start us, length us, event | category | flops | bytes accessed | tf_op | source)
XLA Modules:
  0.0 72.9 jit_solution(1912940777724721757)
XLA Ops:
  0.6 2.5 %gather_rows.1.picked = bf16[32,768]{1,0:T(8,128)(2,1)S(1)} custom-call(s32[32]{0:T(128)} %tok_s.1, bf16[13056,768]{1,0:T(8,128)(2,1)} %embed_h.1), custom_call_target="tpu_custom_call" | custom-call | tf_op jit(solution)/shard_map/gather_rows/pallas_call | solution.py:381
  3.2 56.7 %decoder_layers.1 = (bf16[32,768]{1,0:T(8,128)(2,1)S(1)}, f32[2,32,192]{2,1,0:T(8,128)S(1)}, f32[2,32,192]{2,1,0:T(8,128)S(1)}, bf16[7,4,192,128]{3,2,1,0:T(8,12...) custom-call(s32[32]{0:T(128)} %pos_s.3, ...), custom_call_target="tpu_custom_call" | custom-call | tf_op jit(solution)/shard_map/decoder_layers/pallas_call | solution.py:396
  59.9 12.8 %logits_and_caches.1 = (f32[32,13056]{1,0:T(8,128)}, bf16[2,2,4,4,192,448]{5,4,3,2,1,0:T(8,128)(2,1)}, bf16[2,2,4,4,192,448]{5,4,3,2,1,0:T(8,128)(2,1)}) custom-call(s32[32]{0:T(128)} %pos_s.3, bf16[32,768]{1,0:T(8,128)(2,1)S(1)} %get-tuple-element.12.xf, f32[2,32,192]{2,1,0:T(8,128)S(1)} %get-tuple-element.13.kn, f32[2,32,192]{2,1,0:T(8,128)S(1)} %get-tuple-element.14.vn, ...), custom_call_target="tpu_custom_call" | custom-call | tf_op jit(solution)/shard_map/logits_and_caches/pallas_call | solution.py:421

commit v4 on v3

--- a/solution.py
+++ b/solution.py
@@ -15,7 +15,9 @@
 PARTS = 2
 BLOCK = 2
 VOCAB_CHUNK = 768
-STAGE_SLOTS = 8
+BATCH = 2
+WINDOW = 8
+PER_BATCH = 3
 MIB = 1024 * 1024
 
 
@@ -65,8 +67,8 @@
 
 
 def layers_kernel(pos_s, picked, inb, outb, lnp, bf1, lnf, ptab_h, wqkv_h, wcq_h, wout_h, w1_h, w2_h, sk_h, sv_h, ck_h, cv_h, embed_h,
-                  xo, kn, vn, ext, ring, skv,
-                  x, of, hot, ptab, wqkv, wcq, wout, w1, w2, emb, ar, sem_p, sem_w, sem_s, sem_c, sem_v, sem_es, sem_er, sem_as, sem_ar):
+                  xo, ext, ring, skv,
+                  x, kn, vn, of, hot, newt, ptab, wqkv, wcq, wout, w1, w2, emb, ar, sem_p, sem_w, sem_s, sem_c, sem_v, sem_es, sem_er, sem_as, sem_ar):
     n_layer, n_seq, width = kn.shape
     per_part = n_seq // PARTS
     n_group = per_part // GROUP
@@ -77,6 +79,10 @@
     ctx = skv.shape[-1]
     me = lax.axis_index('tp')
     peers = [lax.rem(me + d, 4) for d in (1, 2, 3)]
+
+    barrier = pltpu.get_barrier_semaphore()
+    for peer in peers:
+        pl.semaphore_signal(barrier, inc=1, device_id={'tp': peer}, device_id_type=MESH)
 
     weights = ((wqkv_h, wqkv), (wcq_h, wcq), (wout_h, wout), (w1_h, w1), (w2_h, w2))
 
@@ -135,9 +141,6 @@
         start_self(0, part)
         start_weights(0, ((2,), (1,))[part])
 
-    barrier = pltpu.get_barrier_semaphore()
-    for peer in peers:
-        pl.semaphore_signal(barrier, inc=1, device_id={'tp': peer}, device_id_type=MESH)
     pl.semaphore_wait(barrier, 3)
     start_cross((0, 1))
 
@@ -269,6 +272,16 @@
         active = (0.5 * pre * (1.0 + lax.erf(pre * (0.5 ** 0.5)))).astype(BF16)
         return dot_nn(active, w2[layer])
 
+    def update(layer, kv):
+        newt[...] = (kn, vn)[kv][layer].T
+        for item in range(layer_items):
+            for u in range(GROUP):
+                b = (item // n_group * GROUP + u) * n_group + item % n_group
+                here = lane == pos_s[b]
+                for r in range(0, width, 16):
+                    column = jnp.broadcast_to(newt[r:r + 16, b:b + 1], (16, ctx)).astype(BF16)
+                    skv[kv, layer, item, u, r:r + 16, :] = jnp.where(here, column, skv[kv, layer, item, u, r:r + 16, :])
+
     stages = (self_stage, cross_stage, mlp_stage)
     def start_ahead(layer, kind, part):
         if kind == 0 and layer == 0:
@@ -293,6 +306,8 @@
                 layer, kind = divmod(step, 3)
                 send(step * PARTS + part, stages[kind](layer, part, rows))
                 start_ahead(layer, kind, part)
+                if part == PARTS - 1 and kind != 1:
+                    update(layer, kind // 2)
     xo[...] = layer_norm(x[...], lnf[0:1, :], lnf[1:2, :])
     for inst in range(n_layer * 3 * PARTS):
         for d in range(3):
@@ -302,38 +317,22 @@
             copy.wait()
 
 
-def tail_kernel(pos_s, xf, kn, vn, ext, ring, skv, logit_h, nk_h, nv_h, lbuf, stage, newt, sem_l, sem_n):
-    _, n_layer, n_chunk, _, width, ctx = skv.shape
-    n_seq = n_chunk * GROUP
+def tail_kernel(xf, ext, ring, skv, logit_h, nk_h, nv_h, lbuf, sem_l, sem_n):
+    _, n_layer, n_chunk, _, _, _ = skv.shape
     n_group = n_chunk // PARTS
     n_vocab = lbuf.shape[0]
     ahead = 2 * SLOTS
     model = xf.shape[1]
     split = model - ext.shape[3]
-    n_write = 2 * n_layer * n_chunk
 
     def l_copy(c):
         return pltpu.make_async_copy(lbuf.at[c], logit_h.at[:, pl.ds(c * VOCAB_CHUNK, VOCAB_CHUNK)], sem_l.at[c])
 
-    def n_copy(i):
-        kv, layer, c = i // (n_layer * n_chunk), i // n_chunk % n_layer, i % n_chunk
-        return pltpu.make_async_copy(stage.at[i % STAGE_SLOTS], (nk_h, nv_h)[kv].at[layer, c // n_group, :, c % n_group], sem_n.at[i % STAGE_SLOTS])
-
-    lane = lax.broadcasted_iota(jnp.int32, (16, ctx), 1)
-
-    def write(i):
-        kv, layer, c = i // (n_layer * n_chunk), i // n_chunk % n_layer, i % n_chunk
-        if c == 0:
-            newt[...] = (kn, vn)[kv][layer].T
-        if i >= STAGE_SLOTS:
-            n_copy(i - STAGE_SLOTS).wait()
-        for s in range(GROUP):
-            b = (c // n_group * GROUP + s) * n_group + c % n_group
-            here = lane == pos_s[b]
-            for r in range(0, width, 16):
-                column = jnp.broadcast_to(newt[r:r + 16, b:b + 1], (16, ctx)).astype(BF16)
-                stage[i % STAGE_SLOTS, s, r:r + 16, :] = jnp.where(here, column, skv[kv, layer, c, s, r:r + 16, :])
-        n_copy(i).start()
+    def n_copies():
+        for kv, out_h in enumerate((nk_h, nv_h)):
+            for layer in range(n_layer):
+                for c in range(n_chunk):
+                    yield pltpu.make_async_copy(skv.at[kv, layer, c], out_h.at[layer, c // n_group, :, c % n_group], sem_n.at[kv, layer, c])
 
     def logit(c):
         kv, slot = chunk_place(c, n_layer * n_chunk)
@@ -343,20 +342,26 @@
             left = ring[kv, slot, :, :, model:model + split].reshape(VOCAB_CHUNK, split)
             right = ext[c - ahead].reshape(VOCAB_CHUNK, model - split)
             lbuf[c] = dot_nt(xf[:, 0:split], left) + dot_nt(xf[:, split:model], right)
-        l_copy(c).start()
-
-    for i in range(STAGE_SLOTS // 2):
-        write(i)
-    for i in range(STAGE_SLOTS // 2, n_write):
-        write(i)
-        if i % 2 and i // 2 < n_vocab:
-            logit(i // 2 - STAGE_SLOTS // 4)
-    for c in range(n_write // 2 - STAGE_SLOTS // 4, n_vocab):
-        logit(c)
+
+    writes = list(n_copies())
+    for copy in writes[:WINDOW]:
+        copy.start()
+    head, tail = 0, WINDOW
+    for first in range(0, n_vocab, BATCH):
+        batch = range(first, min(first + BATCH, n_vocab))
+        for c in batch:
+            logit(c)
+        for c in batch:
+            l_copy(c).start()
+        for _ in range(PER_BATCH):
+            if tail < len(writes):
+                writes[head].wait()
+                writes[tail].start()
+                head, tail = head + 1, tail + 1
     for c in range(n_vocab):
         l_copy(c).wait()
-    for i in range(n_write - STAGE_SLOTS, n_write):
-        n_copy(i).wait()
+    for copy in writes[head:]:
+        copy.wait()
 
 
 def solution(mesh):
@@ -393,21 +398,20 @@
         embed_chunks = embed_table.reshape(n_vocab, GROUP, width, model)
         n_inst = n_layer * 3 * PARTS
         n_item = PARTS * n_group
-        xf, kn, vn, ext, ring, skv = pl.pallas_call(
+        xf, ext, ring, skv = pl.pallas_call(
             layers_kernel,
             out_shape=(
                 pltpu.VMEM((n_seq, model), BF16),
-                pltpu.VMEM((n_layer, n_seq, width), F32),
-                pltpu.VMEM((n_layer, n_seq, width), F32),
                 pltpu.VMEM((n_vocab - 2 * SLOTS, GROUP, width, 128), BF16),
                 pltpu.VMEM((2, SLOTS, GROUP, width, frames), BF16),
                 pltpu.VMEM((2, n_layer, n_item, GROUP, width, ctx), BF16),
             ),
             in_specs=[smem] + [vmem] * 6 + [hbm] * 11,
-            out_specs=(vmem,) * 6,
+            out_specs=(vmem,) * 4,
             scratch_shapes=[
-                pltpu.VMEM((n_seq, model), F32), pltpu.VMEM((n_group, GROUP * width), F32),
-                pltpu.VMEM((n_seq, ctx), F32), pltpu.VMEM(pos_table.shape, BF16),
+                pltpu.VMEM((n_seq, model), F32), pltpu.VMEM((n_layer, n_seq, width), F32), pltpu.VMEM((n_layer, n_seq, width), F32),
+                pltpu.VMEM((n_group, GROUP * width), F32),
+                pltpu.VMEM((n_seq, ctx), F32), pltpu.VMEM((width, n_seq), F32), pltpu.VMEM(pos_table.shape, BF16),
                 pltpu.VMEM(wqkv.shape, BF16), pltpu.VMEM(wcq.shape, BF16), pltpu.VMEM(wout.shape, BF16),
                 pltpu.VMEM(w_fc1.shape, BF16), pltpu.VMEM(w_fc2.shape, BF16),
                 pltpu.VMEM((4, n_seq, model), BF16), pltpu.VMEM((n_inst, 4, n_seq // PARTS, model), F32),
@@ -425,16 +429,15 @@
                 jax.ShapeDtypeStruct(sk.shape, BF16),
                 jax.ShapeDtypeStruct(sv.shape, BF16),
             ),
-            in_specs=[smem] + [vmem] * 6,
+            in_specs=[vmem] * 4,
             out_specs=(hbm, hbm, hbm),
             scratch_shapes=[
                 pltpu.VMEM((n_vocab, n_seq, VOCAB_CHUNK), F32),
-                pltpu.VMEM((STAGE_SLOTS, GROUP, width, ctx), BF16), pltpu.VMEM((width, n_seq), F32),
-                dma((n_vocab,)), dma((STAGE_SLOTS,)),
+                dma((n_vocab,)), dma((2, n_layer, n_item)),
             ],
             compiler_params=pltpu.CompilerParams(vmem_limit_bytes=15 * MIB),
             name='logits_and_caches',
-        )(positions, *(on_chip(z) for z in (xf, kn, vn, ext, ring, skv)))
+        )(*(on_chip(z) for z in (xf, ext, ring, skv)))
         unflat = lambda cache: jnp.transpose(cache.reshape(n_layer, n_seq, n_head, head_dim, ctx), (0, 1, 4, 2, 3))
         return logits, unflat(nk), unflat(nv)
 

time: 73 us -> 69.2 us (0.948)
  Pallas kernels: 72.1 us -> 68.1 us
    pallas_call x1, Pallas kernels: 12.8 us -> 9.27 us  [local_step(): pl.pallas_call(tail_kernel, out_shape=(jax.ShapeDtypeStruct((n_seq, vocab...]
where the time goes in v4:
time: 69.2 us; the launch traced here: 68.9 us
  Pallas kernels  68.1 us (98%)
  between operations  0.81 us (1%)
    pallas_call x1, Pallas kernels, local_step(): pl.pallas_call(layers_kernel, out_shape=(pltpu.VMEM((n_seq, model), BF16)...  56.3 us
    pallas_call x1, Pallas kernels, local_step(): pl.pallas_call(tail_kernel, out_shape=(jax.ShapeDtypeStruct((n_seq, vocab...  9.27 us
    pallas_call x1, Pallas kernels, local_step(): pl.pallas_call(gather_kernel, out_shape=pltpu.VMEM((n_seq, model), BF16),...  2.49 us

profile of v4, /device:TPU:0, one launch (start us, length us, event | category | flops | bytes accessed | tf_op | source)
XLA Modules:
  0.0 68.9 jit_solution(9294798438762612113)
XLA Ops:
  0.6 2.5 %gather_rows.1.picked = bf16[32,768]{1,0:T(8,128)(2,1)S(1)} custom-call(s32[32]{0:T(128)} %tok_s.1, bf16[13056,768]{1,0:T(8,128)(2,1)} %embed_h.1), custom_call_target="tpu_custom_call" | custom-call | tf_op jit(solution)/shard_map/gather_rows/pallas_call | solution.py:386
  3.1 56.3 %decoder_layers.1 = (bf16[32,768]{1,0:T(8,128)(2,1)S(1)}, bf16[7,4,192,128]{3,2,1,0:T(8,128)(2,1)S(1)}, bf16[2,5,4,192,1500]{4,3,2,1,0:T(8,128)(2,1)S(1)}, bf16[2,2,8,4,192,448]{5,4,3,2,1,0:T(8,128)(2,1)S(1)}) custom-call(s32[32]{0:T(128)} %pos_s.1, bf16[32,768]{1,0:T(8,128)(2,1)S(1)} %gather_rows.1.picked, f32[3,3,2,64]{3,2,1,0:T(2,128)} %bitcast.37, ...), custom_call_target="tpu_custom_call" | custom-call | tf_op jit(solution)/shard_map/decoder_layers/pallas_call | solution.py:401
  59.5 9.3 %logits_and_caches.1 = (f32[32,13056]{1,0:T(8,128)}, bf16[2,2,4,4,192,448]{5,4,3,2,1,0:T(8,128)(2,1)}, bf16[2,2,4,4,192,448]{5,4,3,2,1,0:T(8,128)(2,1)}) custom-call(bf16[32,768]{1,0:T(8,128)(2,1)S(1)} %get-tuple-element.10.xf, bf16[7,4,192,128]{3,2,1,0:T(8,128)(2,1)S(1)} %get-tuple-element.11.ext, bf16[2,5,4,192,1500]{4,3,2,1,0:T(8,128)(2,1)S(1)} %get-tuple-element.12.ring, ...), custom_call_target="tpu_custom_call" | custom-call | tf_op jit(solution)/shard_map/logits_and_caches/pallas_call | solution.py:425
